TPU v7x, 256 devices: a whole 4x4x8 slice. The times are simulated.
256 devices in a mesh: grp: 4 (over x), row: 64 (over y, z, core).
Axes of the slice: x: 4, y: 4, z: 8, core: 2. Of those that a mesh axis runs over, the one named last changes fastest.
Arguments:
- snapshots: float32 [229376, 2048], P('row', 'grp'), may hold values from -24 to 24, as said below
- test_block: float32 [229376, 512], P('row', 'grp'), may hold values from -24 to 24, as said below
- start_block: float32 [2048, 64], P('grp'), may hold values from -6 to 6
- start_merge: float32 [256, 64], replicated, may hold values from -6 to 6
Outputs:
- projected: float32 [229376, 512], P('row', 'grp')
Inputs may be any that keep to these rules, and one draw needn't show every extreme that they name: snapshots are float32 values of order one, full rank. test_block holds float32 values of order one.
All inputs are finite; a program needn't handle non-finite values.
Results may differ from a plain program's by a relative error of at most 0.0003.
Values sent between devices are 32-bit elements; how exact they have to be, the bound alone decides.
A program may use at most 64 MiB of HBM per device.

v0:
```python
import functools
import math

import jax
import jax.numpy as jnp
from jax import lax
from jax.sharding import Mesh
from jax.sharding import PartitionSpec as P

ITERS = 6
ROW = ("row_0", "row_1", "row_2")


def in_blocks(array, dim, length):
    shape = array.shape
    blocks = array.reshape(*shape[:dim], length, shape[dim] // length, *shape[dim + 1 :])
    return jnp.moveaxis(blocks, dim, 0)


def sent_and_summed(array, axis, dim):
    length = lax.axis_size(axis)
    blocks = lax.all_to_all(in_blocks(array, dim, length), axis, 0, 0, tiled=True)
    return jnp.sum(blocks, axis=0)


def sum_in_two_steps(array, axes, dim):
    far, near = axes
    blocks = in_blocks(array, dim, lax.axis_size(far))
    nearer = sent_and_summed(blocks, near, dim + 1)
    arrived = lax.all_to_all(nearer, far, split_axis=0, concat_axis=0, tiled=True)
    return arrived.sum(axis=0)


def sent_to_all(array, axis):
    copies = jnp.broadcast_to(array, (lax.axis_size(axis), *array.shape))
    return lax.all_to_all(copies, axis, split_axis=0, concat_axis=0, tiled=True)


def laid_out(blocks, dim):
    blocks = jnp.moveaxis(blocks, 0, dim)
    shape = blocks.shape
    return blocks.reshape(*shape[:dim], shape[dim] * shape[dim + 1], *shape[dim + 2 :])


def gathered_copies(array, axis, dim):
    blocks = sent_to_all(array, axis)
    return laid_out(blocks, dim)


def filled_up(lines, length):
    spare = -lines.shape[0] % length
    if not spare:
        return lines
    return jnp.concatenate([lines, jnp.zeros((spare, *lines.shape[1:]), lines.dtype)])


def nested_sum(array, axes):
    lines = array.reshape(-1, array.shape[-1])
    own = sent_and_summed(filled_up(lines, lax.axis_size(axes)), axes, 0)
    whole = gathered_copies(own, axes, 0)
    return whole[: len(lines)].reshape(array.shape)


def by_axis(array, axes):
    return functools.reduce(lax.psum, axes, array)


def highdot(left, right):
    return jnp.dot(left, right, precision=lax.Precision.HIGHEST, preferred_element_type=jnp.float32)


def orthonormal(tall_block):
    small_gram = highdot(tall_block.T, tall_block)
    lower_factor = jnp.linalg.cholesky(small_gram)
    return lax.linalg.triangular_solve(
        lower_factor, tall_block, left_side=False, lower=True, transpose_a=True
    )


def merge_solve(merged_gram, start_merge):
    merge_coef = orthonormal(start_merge)
    for sweep_index in range(ITERS):
        merge_coef = orthonormal(highdot(merged_gram, merge_coef))
    energy = highdot(merge_coef.T, highdot(merged_gram, merge_coef))
    lower_factor = jnp.linalg.cholesky(energy)
    return lax.linalg.triangular_solve(
        lower_factor, merge_coef, left_side=False, lower=True, transpose_a=True
    )


def on_device(snapshots, test_block, start_block, start_merge):
    rows_dev, snap_width = snapshots.shape
    row_total = rows_dev * lax.axis_size(ROW)
    gram_rows = (
        sum_in_two_steps(highdot(snapshots.T, snapshots), (("row_0", "row_1"), "row_2"), 0)
        / row_total
    )
    iterate = orthonormal(start_block)
    for sweep_index in range(ITERS):
        product = highdot(gram_rows, iterate)
        iterate = orthonormal(gathered_copies(product, ROW, 0))
    group_basis = highdot(snapshots, iterate)
    joined = gathered_copies(group_basis, "grp", 1)
    merged_gram = nested_sum(highdot(joined.T, joined), ROW) / row_total
    merge_coef = merge_solve(merged_gram, start_merge)
    merged_modes = highdot(joined, merge_coef) / math.sqrt(row_total)
    test_coeffs = by_axis(highdot(merged_modes.T, test_block), ROW)
    return highdot(merged_modes, test_coeffs)


def solution(mesh):
    finer = Mesh(
        mesh.devices.reshape(mesh.shape["grp"], 4, 8, 2), ("grp", "row_0", "row_1", "row_2")
    )
    placed = (P(ROW, "grp"), P(ROW, "grp"), P("grp", None), P())
    return jax.shard_map(
        on_device, mesh=finer, in_specs=placed, out_specs=P(ROW, "grp"), check_vma=False
    )
```

profile of v0, /device:TPU:1, one launch (start us, length us, event | category | flops | bytes accessed | tf_op | source)
XLA Modules:
  0.0 490.3 jit_solution(1117492669274309695)
XLA Ops:
  0.0 17.3 %fusion.95 = f32[512,512]{1,0:T(8,128)S(1)} fusion(f32[3584,512]{1,0:T(8,128)} %param.9), kind=kOutput, calls=%fused_computation.176 | convolution fusion | flops 11274289152 | bytes 8388608 | tf_op jit(solution)/shard_map/dot_general | solution.py:69
  17.4 7.4 %all_to_all.55 = f32[2,32,8,512]{3,2,1,0:T(8,128)S(1)} all-to-all(f32[2,32,8,512]{3,2,1,0:T(8,128)S(1)} %bitcast.269), channel_id=1, replica_groups=mesh['grp'=4,'row_0'=4,'row_1'=8,'row_2'=2] {'row_2'}, dimensions={0} | all-to-all | bytes 2097152 | tf_op jit(solution)/shard_map/all_to_all | solution.py:22
  25.7 9.5 %all-to-all-start.1 = ((f32[32,8,512]{2,1,0:T(8,128)}), f32[32,8,512]{2,1,0:T(8,128)S(1)}, u32[]{:S(2)}, u32[]{:S(2)}) async-start(f32[32,8,512]{2,1,0:T(8,128)} %reduce_sum.27), calls=%async_computation.1 | async-start | bytes 1048576 | tf_op jit(solution)/shard_map/all_to_all | solution.py:30
  35.5 5.8 %cholesky.239 = f32[64,64]{1,0:T(8,128)S(1)} custom-call(f32[64,64]{1,0:T(8,128)S(1)} %fusion.58), custom_call_target="Cholesky" | custom-call | tf_op jit(solution)/shard_map/jit(cholesky)/cholesky | solution.py:74
  42.8 4.9 custom-call.21
  49.8 20.0 %all_to_all.56 = f32[64,1,512]{2,1,0:T(1,128)S(1)} all-to-all(f32[64,1,512]{2,1,0:T(1,128)S(1)} %reshape.113), channel_id=1, replica_groups=mesh['grp'=4,'row_0'=4,'row_1'=8,'row_2'=2] {'row_0','row_1','row_2'}, dimensions={0} | all-to-all | bytes 262144 | tf_op jit(solution)/shard_map/all_to_all | solution.py:36
  72.1 5.8 %cholesky.250 = f32[64,64]{1,0:T(8,128)S(1)} custom-call(f32[64,64]{1,0:T(8,128)S(1)} %fusion.56), custom_call_target="Cholesky" | custom-call | tf_op jit(solution)/shard_map/jit(cholesky)/cholesky | solution.py:74
  79.4 4.9 custom-call.22
  85.2 15.0 %all_to_all.57 = f32[64,1,512]{2,1,0:T(1,128)S(1)} all-to-all(f32[64,1,512]{2,1,0:T(1,128)S(1)} %reshape.115), channel_id=1, replica_groups=mesh['grp'=4,'row_0'=4,'row_1'=8,'row_2'=2] {'row_0','row_1','row_2'}, dimensions={0} | all-to-all | bytes 262144 | tf_op jit(solution)/shard_map/all_to_all | solution.py:36
  101.9 5.8 %cholesky.261 = f32[64,64]{1,0:T(8,128)S(1)} custom-call(f32[64,64]{1,0:T(8,128)S(1)} %fusion.54), custom_call_target="Cholesky" | custom-call | tf_op jit(solution)/shard_map/jit(cholesky)/cholesky | solution.py:74
  109.3 4.9 custom-call.23
  115.0 15.0 %all_to_all.58 = f32[64,1,512]{2,1,0:T(1,128)S(1)} all-to-all(f32[64,1,512]{2,1,0:T(1,128)S(1)} %reshape.117), channel_id=1, replica_groups=mesh['grp'=4,'row_0'=4,'row_1'=8,'row_2'=2] {'row_0','row_1','row_2'}, dimensions={0} | all-to-all | bytes 262144 | tf_op jit(solution)/shard_map/all_to_all | solution.py:36
  131.8 5.8 %cholesky.272 = f32[64,64]{1,0:T(8,128)S(1)} custom-call(f32[64,64]{1,0:T(8,128)S(1)} %fusion.52), custom_call_target="Cholesky" | custom-call | tf_op jit(solution)/shard_map/jit(cholesky)/cholesky | solution.py:74
  139.1 4.9 custom-call.24
  144.9 15.2 %all_to_all.59 = f32[64,1,512]{2,1,0:T(1,128)S(1)} all-to-all(f32[64,1,512]{2,1,0:T(1,128)S(1)} %reshape.119), channel_id=1, replica_groups=mesh['grp'=4,'row_0'=4,'row_1'=8,'row_2'=2] {'row_0','row_1','row_2'}, dimensions={0} | all-to-all | bytes 262144 | tf_op jit(solution)/shard_map/all_to_all | solution.py:36
  161.8 5.8 %cholesky.283 = f32[64,64]{1,0:T(8,128)S(1)} custom-call(f32[64,64]{1,0:T(8,128)S(1)} %fusion.50), custom_call_target="Cholesky" | custom-call | tf_op jit(solution)/shard_map/jit(cholesky)/cholesky | solution.py:74
  169.2 4.9 custom-call.25
  174.9 15.0 %all_to_all.60 = f32[64,1,512]{2,1,0:T(1,128)S(1)} all-to-all(f32[64,1,512]{2,1,0:T(1,128)S(1)} %reshape.121), channel_id=1, replica_groups=mesh['grp'=4,'row_0'=4,'row_1'=8,'row_2'=2] {'row_0','row_1','row_2'}, dimensions={0} | all-to-all | bytes 262144 | tf_op jit(solution)/shard_map/all_to_all | solution.py:36
  191.7 5.8 %cholesky.294 = f32[64,64]{1,0:T(8,128)S(1)} custom-call(f32[64,64]{1,0:T(8,128)S(1)} %fusion.48), custom_call_target="Cholesky" | custom-call | tf_op jit(solution)/shard_map/jit(cholesky)/cholesky | solution.py:74
  199.0 4.9 custom-call.26
  204.8 15.2 %all_to_all.61 = f32[64,1,512]{2,1,0:T(1,128)S(1)} all-to-all(f32[64,1,512]{2,1,0:T(1,128)S(1)} %reshape.123), channel_id=1, replica_groups=mesh['grp'=4,'row_0'=4,'row_1'=8,'row_2'=2] {'row_0','row_1','row_2'}, dimensions={0} | all-to-all | bytes 262144 | tf_op jit(solution)/shard_map/all_to_all | solution.py:36
  221.8 5.8 %cholesky.305 = f32[64,64]{1,0:T(8,128)S(1)} custom-call(f32[64,64]{1,0:T(8,128)S(1)} %fusion.46), custom_call_target="Cholesky" | custom-call | tf_op jit(solution)/shard_map/jit(cholesky)/cholesky | solution.py:74
  229.0 4.9 custom-call.27
  234.3 9.2 %convolution_bitcast_fusion = f32[3584,64]{0,1:T(8,128)S(1)} fusion(f32[512,64]{0,1:T(8,128)S(1)} %convolution_bitcast_fusion.1, f32[3584,512]{1,0:T(8,128)} %param.9), kind=kOutput, calls=%fused_computation.1 | convolution fusion | flops 1409286144 | bytes 8388608 | tf_op jit(solution)/shard_map/dot_general | solution.py:69
  244.0 46.2 %all_to_all.62 = f32[4,3584,64]{1,2,0:T(8,128)} all-to-all(f32[4,3584,64]{1,2,0:T(8,128)S(1)} %broadcast_in_dim.31), channel_id=1, replica_groups=mesh['grp'=4,'row_0'=4,'row_1'=8,'row_2'=2] {'grp'}, dimensions={0} | all-to-all | bytes 7340032 | tf_op jit(solution)/shard_map/all_to_all | solution.py:36
  290.2 5.2 %dot_general.125 = f32[64,4,3584]{2,1,0:T(4,128)} reshape(f32[256,3584]{1,0:T(8,128)} %bitcast.266) | data formatting | bytes 7340032 | tf_op jit(solution)/shard_map/dot_general | solution.py:69
  295.4 7.1 %fusion = f32[64,4,256]{2,0,1:T(8,128)S(1)} fusion(f32[3584,256,1]{0,1,2:T(8,128)} %bitcast.267, f32[64,4,3584]{2,1,0:T(4,128)} %dot_general.125), kind=kOutput, calls=%fused_computation.2 | convolution fusion | flops 2818572288 | bytes 7602176 | tf_op jit(solution)/shard_map/dot_general | solution.py:69
  303.3 6.2 %all-to-all-start.9 = ((f32[64,4,256]{2,1,0:T(4,128)}), f32[64,4,256]{2,1,0:T(4,128)S(1)}, u32[]{:S(2)}, u32[]{:S(2)}) async-start(f32[64,4,256]{2,1,0:T(4,128)} %copy.110), calls=%async_computation.9 | async-start | bytes 524288 | tf_op jit(solution)/shard_map/all_to_all | solution.py:22
  309.8 5.8 %cholesky.316 = f32[64,64]{1,0:T(8,128)S(1)} custom-call(f32[64,64]{1,0:T(8,128)S(1)} %fusion.44), custom_call_target="Cholesky" | custom-call | tf_op jit(solution)/shard_map/jit(cholesky)/cholesky | solution.py:74
  315.7 5.8 %all-to-all-done.9 = f32[64,4,256]{2,1,0:T(4,128)S(1)} async-done(((f32[64,4,256]{2,1,0:T(4,128)}), f32[64,4,256]{2,1,0:T(4,128)S(1)}, u32[]{:S(2)}, u32[]{:S(2)}) %all-to-all-start.9) | async-done | bytes 262176 | tf_op jit(solution)/shard_map/all_to_all | solution.py:22
  322.3 6.5 %all-to-all-start.10 = ((f32[64,4,256]{2,1,0:T(4,128)}), f32[64,4,256]{2,1,0:T(4,128)S(1)}, u32[]{:S(2)}, u32[]{:S(2)}) async-start(f32[64,4,256]{2,1,0:T(4,128)} %broadcast_in_dim.32), calls=%async_computation.10 | async-start | bytes 524288 | tf_op jit(solution)/shard_map/all_to_all | solution.py:36
  330.0 4.9 custom-call.28
  335.2 5.1 %all-to-all-done.10 = f32[64,4,256]{2,1,0:T(4,128)S(1)} async-done(((f32[64,4,256]{2,1,0:T(4,128)}), f32[64,4,256]{2,1,0:T(4,128)S(1)}, u32[]{:S(2)}, u32[]{:S(2)}) %all-to-all-start.10) | async-done | bytes 262176 | tf_op jit(solution)/shard_map/all_to_all | solution.py:36
  341.2 5.8 %cholesky.327 = f32[64,64]{1,0:T(8,128)S(1)} custom-call(f32[64,64]{1,0:T(8,128)S(1)} %fusion.42), custom_call_target="Cholesky" | custom-call | tf_op jit(solution)/shard_map/jit(cholesky)/cholesky | solution.py:74
  348.4 4.9 custom-call.29
  354.2 5.8 %cholesky.338 = f32[64,64]{1,0:T(8,128)S(1)} custom-call(f32[64,64]{1,0:T(8,128)S(1)} %fusion.40), custom_call_target="Cholesky" | custom-call | tf_op jit(solution)/shard_map/jit(cholesky)/cholesky | solution.py:74
  361.4 4.9 custom-call.30
  367.3 5.8 %cholesky.349 = f32[64,64]{1,0:T(8,128)S(1)} custom-call(f32[64,64]{1,0:T(8,128)S(1)} %fusion.38), custom_call_target="Cholesky" | custom-call | tf_op jit(solution)/shard_map/jit(cholesky)/cholesky | solution.py:74
  374.5 4.9 custom-call.31
  380.3 5.8 %cholesky.360 = f32[64,64]{1,0:T(8,128)S(1)} custom-call(f32[64,64]{1,0:T(8,128)S(1)} %fusion.36), custom_call_target="Cholesky" | custom-call | tf_op jit(solution)/shard_map/jit(cholesky)/cholesky | solution.py:74
  393.4 5.8 %cholesky.371 = f32[64,64]{1,0:T(8,128)S(1)} custom-call(f32[64,64]{1,0:T(8,128)S(1)} %fusion.34), custom_call_target="Cholesky" | custom-call | tf_op jit(solution)/shard_map/jit(cholesky)/cholesky | solution.py:74
  400.6 5.0 %custom-call.33 = f32[1,64,64]{1,2,0:T(8,128)S(1)} custom-call(f32[1,64,64]{2,1,0:T(8,128)S(1)} %fusion.26), custom_call_target="InvertDiagBlocksLowerTriangular" | custom-call | tf_op jit(solution)/shard_map/triangular_solve/custom-call.2 | solution.py:75
  406.5 5.8 %cholesky.382 = f32[64,64]{1,0:T(8,128)S(1)} custom-call(f32[64,64]{1,0:T(8,128)S(1)} %fusion.32), custom_call_target="Cholesky" | custom-call | tf_op jit(solution)/shard_map/jit(cholesky)/cholesky | solution.py:74
  419.6 5.8 %cholesky.393 = f32[64,64]{1,0:T(8,128)S(1)} custom-call(f32[64,64]{1,0:T(8,128)S(1)} %fusion.30), custom_call_target="Cholesky" | custom-call | tf_op jit(solution)/shard_map/jit(cholesky)/cholesky | solution.py:85
  426.7 4.9 custom-call.35
  437.7 13.2 %psum.21 = f32[64,128]{1,0:T(8,128)S(1)} all-reduce(f32[64,128]{1,0:T(8,128)S(1)} %fusion.112), channel_id=1, replica_groups=mesh['grp'=4,'row_0'=4,'row_1'=8,'row_2'=2] {'row_0'}, use_global_device_ids=true, to_apply=%region_5.9 | all-reduce | flops 8192 | bytes 65536 | tf_op jit(solution)/shard_map/psum | solution.py:65
  450.9 20.9 %psum.22 = f32[64,128]{1,0:T(8,128)S(1)} all-reduce(f32[64,128]{1,0:T(8,128)S(1)} %psum.21), channel_id=1, replica_groups=mesh['grp'=4,'row_0'=4,'row_1'=8,'row_2'=2] {'row_1'}, use_global_device_ids=true, to_apply=%region_6.10 | all-reduce | flops 8192 | bytes 65536 | tf_op jit(solution)/shard_map/psum | solution.py:65
  471.8 14.1 %psum.23 = f32[64,128]{1,0:T(8,128)S(1)} all-reduce(f32[64,128]{1,0:T(8,128)S(1)} %psum.22), channel_id=1, replica_groups=mesh['grp'=4,'row_0'=4,'row_1'=8,'row_2'=2] {'row_2'}, use_global_device_ids=true, to_apply=%region_7.11 | all-reduce | flops 8192 | bytes 65536 | tf_op jit(solution)/shard_map/psum | solution.py:65
  (164 shorter events, 68.7 us)
Async XLA Ops:
  0.0 436.4 %copy-start = (f32[3584,128]{1,0:T(8,128)S(1)}, f32[3584,128]{1,0:T(8,128)}, u32[]{:S(2)}) copy-start(f32[3584,128]{1,0:T(8,128)} %param.10) | copy-start | bytes 5505028
  17.3 17.9 %copy-start.1 = (f32[512,64]{0,1:T(8,128)S(1)}, f32[512,64]{0,1:T(8,128)}, u32[]{:S(2)}) copy-start(f32[512,64]{0,1:T(8,128)} %param.11) | copy-start | bytes 393220
  25.7 23.7 %all-to-all-start.1 = ((f32[32,8,512]{2,1,0:T(8,128)}), f32[32,8,512]{2,1,0:T(8,128)S(1)}, u32[]{:S(2)}, u32[]{:S(2)}) async-start(f32[32,8,512]{2,1,0:T(8,128)} %reduce_sum.27), calls=%async_computation.1 | async-start | bytes 1048576 | tf_op jit(solution)/shard_map/all_to_all | solution.py:30
  295.4 14.1 %copy-start.2 = (f32[256,64]{0,1:T(8,128)S(1)}, f32[256,64]{0,1:T(8,128)}, u32[]{:S(2)}) copy-start(f32[256,64]{0,1:T(8,128)} %param.12) | copy-start | bytes 196612
  303.3 18.1 %all-to-all-start.9 = ((f32[64,4,256]{2,1,0:T(4,128)}), f32[64,4,256]{2,1,0:T(4,128)S(1)}, u32[]{:S(2)}, u32[]{:S(2)}) async-start(f32[64,4,256]{2,1,0:T(4,128)} %copy.110), calls=%async_computation.9 | async-start | bytes 524288 | tf_op jit(solution)/shard_map/all_to_all | solution.py:22
  322.3 18.0 %all-to-all-start.10 = ((f32[64,4,256]{2,1,0:T(4,128)}), f32[64,4,256]{2,1,0:T(4,128)S(1)}, u32[]{:S(2)}, u32[]{:S(2)}) async-start(f32[64,4,256]{2,1,0:T(4,128)} %broadcast_in_dim.32), calls=%async_computation.10 | async-start | bytes 524288 | tf_op jit(solution)/shard_map/all_to_all | solution.py:36
where the time goes:
time: 499 us; the launch traced here: 490 us
  blocking collectives  197 us (39%)
  other arithmetic  189 us (38%)
  matrix products  57.8 us (12%)
  starting transfers between devices  22.2 us (4%)
  waiting for transfers between devices  12.2 us (2%)
  local copies, waits for them, and re-layouts  11.1 us (2%)
    all_to_all x7, blocking collectives, sent_to_all(): return lax.all_to_all(copies, axis, split_axis=0, concat_axis=0, tiled=True)  142 us
    another operation x42, other arithmetic, orthonormal(): lower_factor = jnp.linalg.cholesky(small_gram)  91.8 us
    another operation x28, other arithmetic, orthonormal(): lax.linalg.triangular_solve(lower_factor, tall_block, left_side=False, lo...  78 us
    dot_general x34, matrix products, highdot(): jnp.dot(left, right, precision=lax.Precision.HIGHEST, preferred_element_t...  52.6 us
    psum x3, blocking collectives, by_axis(): return functools.reduce(lax.psum, axes, array)  48.2 us
  transfers between devices with their start and end apart: 3, of which 3 were waited for; matrix products, arithmetic and copies ran while one was open for 5% of the time, Pallas kernels for 0%

commit v1 on v0

v1 whole, which is shorter than its diff:
```python
import functools

import jax
import jax.numpy as jnp
from jax import lax
from jax.experimental import pallas as pl
from jax.experimental.pallas import tpu as pltpu
from jax.sharding import Mesh
from jax.sharding import PartitionSpec as P

ITERS = 6
RANK = 64
ROW = ("row_0", "row_1", "row_2")
MESH = pl.DeviceIdType.MESH
F32, BF16 = jnp.float32, jnp.bfloat16
NT = (((1,), (1,)), ((), ()))
TN = (((0,), (0,)), ((), ()))
NN = (((1,), (0,)), ((), ()))
VMEM = pl.BlockSpec(memory_space=pltpu.VMEM)
GRAM_ROWS = 1536
MERGE_ROWS = 1024


def split(x):
    high = x.astype(BF16)
    return high, (x - high.astype(F32)).astype(BF16)


def bdot(a, b, dims):
    return lax.dot_general(a, b, dims, preferred_element_type=F32)


def fdot(a, b, dims=NN):
    return lax.dot_general(
        a, b, dims, precision=lax.Precision.HIGHEST, preferred_element_type=F32
    )


def lower_inverse(small):
    rows8 = lax.broadcasted_iota(jnp.int32, (8, 128), 0)
    row, lane = (lax.broadcasted_iota(jnp.int32, (64, 64), d) for d in (0, 1))
    joint = jnp.concatenate([jnp.where(row == lane, 1.0, 0.0), small], axis=1)
    bands = [joint[8 * k : 8 * k + 8, :] for k in range(8)]
    done, least, most = [], None, None
    for k in range(8):
        first = 64 + 8 * k
        cols = [
            [jnp.broadcast_to(bands[i][:, first + c : first + c + 1], (8, 128)) for c in range(8)]
            for i in range(k, 8)
        ]
        line = [jnp.broadcast_to(bands[k][a : a + 1, :], (8, 128)) for a in range(8)]
        piv = [[jnp.broadcast_to(cols[0][c][a : a + 1, :], (8, 128)) for c in range(a + 1)] for a in range(8)]
        inv, low = [None] * 8, [[None] * 8 for _ in range(8)]
        for a in range(8):
            inv[a] = 1.0 / piv[a][a]
            for c in range(a + 1, 8):
                low[c][a] = piv[c][a] * inv[a]
            for c in range(a + 1, 8):
                line[c] = line[c] - low[c][a] * line[a]
                for e in range(a + 1, c + 1):
                    piv[c][e] = piv[c][e] - low[c][a] * piv[e][a]
        band, diag = line[0], piv[0][0]
        for a in range(1, 8):
            band = jnp.where(rows8 == a, line[a], band)
            diag = jnp.where(rows8 == a, piv[a][a], diag)
        done.append(band * lax.rsqrt(diag))
        least = diag if least is None else jnp.minimum(least, diag)
        most = diag if most is None else jnp.maximum(most, diag)
        if k < 7:
            back = [line[a] * inv[a] for a in range(8)]
            for a in range(7, -1, -1):
                for c in range(a):
                    back[c] = back[c] - low[a][c] * back[a]
            for i in range(k + 1, 8):
                rest = bands[i]
                for a in range(8):
                    rest = rest - cols[i - k][a] * back[a]
                bands[i] = rest
    return jnp.concatenate(done, axis=0)[:, :64], jnp.min(least), jnp.max(most)


def orth_rows(block):
    inverse, least, most = lower_inverse(fdot(block, block, NT))
    return fdot(inverse, block), least / most


def sweeps(start, gram, out_ref, floor, last_floor):
    block, fine = start, None
    for pair in range(ITERS // 2):
        block, ratio = orth_rows(fdot(fdot(block, gram), gram))
        ok = ratio > (last_floor if pair == ITERS // 2 - 1 else floor)
        fine = ok if fine is None else jnp.logical_and(fine, ok)
    out_ref[...] = block

    @pl.when(jnp.logical_not(fine))
    def _():
        out_ref[...] = orth_rows(start)[0]

        def one(_, carry):
            out_ref[...] = orth_rows(fdot(out_ref[...], gram))[0]
            return carry

        lax.fori_loop(0, ITERS, one, 0)


def gram_kernel(x_ref, out_ref, first, second):
    step = pl.program_id(0)
    high, low = split(x_ref[...])
    one = bdot(high, high, TN)
    two = bdot(high, low, TN)

    @pl.when(step == 0)
    def _():
        first[...] = one
        second[...] = two

    @pl.when(step > 0)
    def _():
        first[...] = first[...] + one
        second[...] = second[...] + two

    @pl.when(step == pl.num_programs(0) - 1)
    def _():
        for at, (i, j) in enumerate(((0, 0), (0, 1), (1, 1))):
            block = (
                first[256 * i : 256 * i + 256, 256 * j : 256 * j + 256]
                + second[256 * i : 256 * i + 256, 256 * j : 256 * j + 256]
                + second[256 * j : 256 * j + 256, 256 * i : 256 * i + 256].T
            )
            for h in range(2):
                out_ref[512 * at + 256 * h : 512 * at + 256 * h + 256, :] = block[:, 128 * h : 128 * h + 128]


def partial_gram(snapshots):
    rows = snapshots.shape[0]
    return pl.pallas_call(
        gram_kernel,
        grid=(rows // 896,),
        in_specs=[pl.BlockSpec((896, 512), lambda i: (i, 0))],
        out_specs=pl.BlockSpec((GRAM_ROWS, 128), lambda i: (0, 0)),
        out_shape=jax.ShapeDtypeStruct((GRAM_ROWS, 128), F32),
        scratch_shapes=[pltpu.VMEM((512, 512), F32), pltpu.VMEM((512, 512), F32)],
        cost_estimate=pl.CostEstimate(flops=4 * rows * 512 * 512, bytes_accessed=rows * 2048, transcendentals=0),
        name="partial_gram",
    )(snapshots)


def sum_kernel(total, in_ref, out_ref, got1, sum1, got2, sum2, got3, send1, recv1, send2, recv2, send3, recv3):
    grp = lax.axis_index("grp")
    y, z, c = (lax.axis_index(name) for name in ROW)
    half, quarter, piece = total // 2, total // 8, total // 64
    mate = (grp, y, z, 1 - c)

    def y_peer(d):
        return lax.rem(y + d, 4)

    def z_peer(d):
        return lax.rem(z + d, 8)

    barrier = pltpu.get_barrier_semaphore()
    pl.semaphore_signal(barrier, inc=1, device_id=mate, device_id_type=MESH)
    for d in range(1, 4):
        pl.semaphore_signal(barrier, inc=1, device_id=(grp, y_peer(d), z, c), device_id_type=MESH)
    for d in range(1, 8):
        pl.semaphore_signal(barrier, inc=1, device_id=(grp, y, z_peer(d), c), device_id_type=MESH)
    pl.semaphore_wait(barrier, 11)

    def rows(start, size):
        return pl.ds(pl.multiple_of(start, 8), size)

    def copy(src, dst, send, recv, device):
        made = pltpu.make_async_remote_copy(
            src_ref=src, dst_ref=dst, send_sem=send, recv_sem=recv, device_id=device, device_id_type=MESH
        )
        made.start()
        return made

    copy(in_ref.at[rows((1 - c) * half, half)], got1, send1.at[0], recv1.at[0], mate).wait()
    sum1[...] = in_ref[rows(c * half, half), :] + got1[...]
    copies = [
        copy(sum1.at[rows(y_peer(d) * quarter, quarter)], got2.at[d - 1], send2.at[d - 1], recv2.at[d - 1],
             (grp, y_peer(d), z, c))
        for d in range(1, 4)
    ]
    for made in copies:
        made.wait()
    sum2[...] = sum1[rows(y * quarter, quarter), :] + got2[0] + got2[1] + got2[2]
    copies = [
        copy(sum2.at[rows(z_peer(d) * piece, piece)], got3.at[d - 1], send3.at[d - 1], recv3.at[d - 1],
             (grp, y, z_peer(d), c))
        for d in range(1, 8)
    ]
    for made in copies:
        made.wait()
    own = c * half + y * quarter + z * piece
    acc = sum2[rows(z * piece, piece), :]
    for d in range(7):
        acc = acc + got3[d]
    out_ref[rows(own, piece), :] = acc
    mine = out_ref.at[rows(own, piece)]
    copies = [
        copy(mine, mine, send3.at[6 + d], recv3.at[6 + d], (grp, y, z_peer(d), c)) for d in range(1, 8)
    ]
    for made in copies:
        made.wait()
    mine = out_ref.at[rows(c * half + y * quarter, quarter)]
    copies = [
        copy(mine, mine, send2.at[2 + d], recv2.at[2 + d], (grp, y_peer(d), z, c)) for d in range(1, 4)
    ]
    for made in copies:
        made.wait()
    mine = out_ref.at[rows(c * half, half)]
    copy(mine, mine, send1.at[1], recv1.at[1], mate).wait()


def sum_over_rows(array, number):
    total = array.shape[0]
    dma = pltpu.SemaphoreType.DMA
    return pl.pallas_call(
        functools.partial(sum_kernel, total),
        in_specs=[VMEM],
        out_specs=VMEM,
        out_shape=jax.ShapeDtypeStruct((total, 128), F32),
        scratch_shapes=[
            pltpu.VMEM((total // 2, 128), F32),
            pltpu.VMEM((total // 2, 128), F32),
            pltpu.VMEM((3, total // 8, 128), F32),
            pltpu.VMEM((total // 8, 128), F32),
            pltpu.VMEM((7, total // 64, 128), F32),
            dma((2,)), dma((2,)), dma((6,)), dma((6,)), dma((14,)), dma((14,)),
        ],
        compiler_params=pltpu.CompilerParams(collective_id=number, has_side_effects=True),
        name=f"sum_over_rows_{number}",
    )(array)


def basis_kernel(row_total, gram_ref, start_ref, x_ref, out_ref, gram, iterate, high_low):
    @pl.when(pl.program_id(0) == 0)
    def _():
        for at, (i, j) in enumerate(((0, 0), (0, 1), (1, 1))):
            for h in range(2):
                block = gram_ref[512 * at + 256 * h : 512 * at + 256 * h + 256, :] * (1.0 / row_total)
                gram[256 * i : 256 * i + 256, 256 * j + 128 * h : 256 * j + 128 * h + 128] = block
        gram[256:512, 0:256] = gram[0:256, 256:512].T
        sweeps(start_ref[...].T, gram[...], iterate, 1e-5, 5e-4)
        high, low = split(iterate[...])
        high_low[0:RANK, :] = high
        high_low[RANK:, :] = low

    high, low = split(x_ref[...])
    both = bdot(high_low[...], high, NT)
    out_ref[...] = both[:RANK] + both[RANK:] + bdot(high_low[0:RANK, :], low, NT)


def group_basis(gram, start_block, snapshots, row_total):
    rows = snapshots.shape[0]
    return pl.pallas_call(
        functools.partial(basis_kernel, row_total),
        grid=(rows // 512,),
        in_specs=[
            pl.BlockSpec((GRAM_ROWS, 128), lambda i: (0, 0)),
            pl.BlockSpec((512, RANK), lambda i: (0, 0)),
            pl.BlockSpec((512, 512), lambda i: (i, 0)),
        ],
        out_specs=pl.BlockSpec((RANK, 512), lambda i: (0, i)),
        out_shape=jax.ShapeDtypeStruct((RANK, rows), F32),
        scratch_shapes=[pltpu.VMEM((512, 512), F32), pltpu.VMEM((RANK, 512), F32), pltpu.VMEM((2 * RANK, 512), BF16)],
        name="group_basis",
    )(gram, start_block, snapshots)


def gather_kernel(in_ref, out_ref, send_r, recv_r, send_l, recv_l, send_f, recv_f):
    g = lax.axis_index("grp")
    y, z, c = (lax.axis_index(name) for name in ROW)
    right, left = lax.rem(g + 1, 4), lax.rem(g + 3, 4)
    part = in_ref.shape[1] // 4
    barrier = pltpu.get_barrier_semaphore()
    for peer in (right, left):
        pl.semaphore_signal(barrier, inc=1, device_id=(peer, y, z, c), device_id_type=MESH)
    pl.semaphore_wait(barrier, 2)

    def place(block, q):
        return out_ref.at[pl.ds(pl.multiple_of(block * RANK, 8), RANK), pl.ds(q * part, part)]

    def copy(src, dst, send, recv, peer):
        return pltpu.make_async_remote_copy(
            src_ref=src, dst_ref=dst, send_sem=send, recv_sem=recv, device_id=(peer, y, z, c), device_id_type=MESH
        )

    to_right = [copy(in_ref.at[:, pl.ds(q * part, part)], place(g, q), send_r.at[q], recv_r.at[q], right) for q in range(4)]
    to_left = [copy(in_ref.at[:, pl.ds(q * part, part)], place(g, q), send_l.at[q], recv_l.at[q], left) for q in range(4)]
    for q in range(4):
        to_right[q].start()
        to_left[(q + 2) % 4].start()
    out_ref[pl.ds(pl.multiple_of(g * RANK, 8), RANK), :] = in_ref[...]
    on = [copy(place(left, q), place(left, q), send_f.at[q], recv_f.at[q], right) for q in range(2)]
    on += [copy(place(right, q), place(right, q), send_f.at[q], recv_f.at[q], left) for q in (2, 3)]
    for q in range(2):
        to_right[q].wait_recv()
        on[q].start()
        to_left[q + 2].wait_recv()
        on[q + 2].start()
    for q in range(2):
        to_right[q + 2].wait_recv()
        to_left[q].wait_recv()
    for made in on:
        made.wait_recv()
    for made in to_right + to_left + on:
        made.wait_send()


def gathered(basis, number):
    rows = basis.shape[1]
    dma = pltpu.SemaphoreType.DMA
    return pl.pallas_call(
        gather_kernel,
        in_specs=[VMEM],
        out_specs=VMEM,
        out_shape=jax.ShapeDtypeStruct((4 * RANK, rows), F32),
        scratch_shapes=[dma((4,))] * 6,
        compiler_params=pltpu.CompilerParams(collective_id=number, has_side_effects=True),
        name="gathered",
    )(basis)


def merge_kernel(joined_ref, test_ref, out_ref, first, second, third):
    step = pl.program_id(0)

    @pl.when(step == 0)
    def _():
        first[...] = jnp.zeros_like(first)
        second[...] = jnp.zeros_like(second)
        third[...] = jnp.zeros_like(third)

    high, low = split(joined_ref[...])
    first[...] += bdot(high, high, NT)
    second[...] += bdot(high, low, NT)
    test_high, test_low = split(test_ref[...])
    third[...] += bdot(high, test_high, NN) + bdot(high, test_low, NN) + bdot(low, test_high, NN)

    @pl.when(step == pl.num_programs(0) - 1)
    def _():
        merged = first[...] + second[...] + second[...].T
        for h in range(2):
            out_ref[256 * h : 256 * h + 256, :] = merged[:, 128 * h : 128 * h + 128]
        out_ref[512:768, :] = third[...]
        out_ref[768:, :] = jnp.zeros((MERGE_ROWS - 768, 128), F32)


def partial_merge(joined, test_block):
    wide, rows = joined.shape
    return pl.pallas_call(
        merge_kernel,
        grid=(rows // 512,),
        in_specs=[
            pl.BlockSpec((wide, 512), lambda i: (0, i)),
            pl.BlockSpec((512, 128), lambda i: (i, 0)),
        ],
        out_specs=pl.BlockSpec((MERGE_ROWS, 128), lambda i: (0, 0)),
        out_shape=jax.ShapeDtypeStruct((MERGE_ROWS, 128), F32),
        scratch_shapes=[pltpu.VMEM((256, 256), F32), pltpu.VMEM((256, 256), F32), pltpu.VMEM((256, 128), F32)],
        name="partial_merge",
    )(joined, test_block)


def project_kernel(row_total, merge_ref, start_ref, joined_ref, out_ref, merged, iterate, factor):
    @pl.when(pl.program_id(0) == 0)
    def _():
        for h in range(2):
            merged[:, 128 * h : 128 * h + 128] = merge_ref[256 * h : 256 * h + 256, :] * (1.0 / row_total)
        sweeps(start_ref[...].T, merged[...], iterate, 3e-6, 3e-6)
        coef = iterate[...]
        energy = fdot(fdot(coef, merged[...]), coef, NT)
        coef = fdot(lower_inverse(energy)[0], coef)
        test_coeffs = fdot(coef, merge_ref[512:768, :]) * (1.0 / row_total)
        high, low = split(fdot(coef, test_coeffs, TN))
        factor[0] = high
        factor[1] = low

    high, low = split(joined_ref[...])
    out_ref[...] = bdot(high, factor[0], TN) + bdot(high, factor[1], TN) + bdot(low, factor[0], TN)


def project(merge, start_merge, joined, row_total):
    wide, rows = joined.shape
    return pl.pallas_call(
        functools.partial(project_kernel, row_total),
        grid=(rows // 512,),
        in_specs=[
            pl.BlockSpec((MERGE_ROWS, 128), lambda i: (0, 0)),
            pl.BlockSpec((256, RANK), lambda i: (0, 0)),
            pl.BlockSpec((wide, 512), lambda i: (0, i)),
        ],
        out_specs=pl.BlockSpec((512, 128), lambda i: (i, 0)),
        out_shape=jax.ShapeDtypeStruct((rows, 128), F32),
        scratch_shapes=[pltpu.VMEM((256, 256), F32), pltpu.VMEM((RANK, 256), F32), pltpu.VMEM((2, 256, 128), BF16)],
        name="project",
    )(merge, start_merge, joined)


def on_device(snapshots, test_block, start_block, start_merge):
    row_total = snapshots.shape[0] * 64
    gram = sum_over_rows(partial_gram(snapshots), 0)
    basis = group_basis(gram, start_block, snapshots, row_total)
    joined = gathered(basis, 1)
    merge = sum_over_rows(partial_merge(joined, test_block), 2)
    return project(merge, start_merge, joined, row_total)


def solution(mesh):
    finer = Mesh(
        mesh.devices.reshape(mesh.shape["grp"], 4, 8, 2), ("grp", "row_0", "row_1", "row_2")
    )
    placed = (P(ROW, "grp"), P(ROW, "grp"), P("grp", None), P())
    return jax.shard_map(
        on_device, mesh=finer, in_specs=placed, out_specs=P(ROW, "grp"), check_vma=False
    )
```

time: 499 us -> 207 us (0.41); the launches traced: 490 us -> 207 us
  Pallas kernels: 0 us -> 203 us
  blocking collectives: 197 us -> 0 us
  other arithmetic: 189 us -> 0 us
  matrix products: 57.8 us -> 0 us
  starting transfers between devices: 22.2 us -> 0 us
  waiting for transfers between devices: 12.2 us -> 0 us
  local copies, waits for them, and re-layouts: 11.1 us -> 3.33 us
    pallas_call x0 -> x7, Pallas kernels: none -> 203 us  [the longest x2 66.8 us: sum_over_rows(): pl.pallas_call(functools.partial(sum_kernel, total), in_specs=[VMEM], out...]
    another operation x75 -> x0, other arithmetic: 182 us -> none  [the longest x42 91.8 us: orthonormal(): lower_factor = jnp.linalg.cholesky(small_gram)]
    all_to_all x8 -> x0, blocking collectives: 149 us -> none  [the longest x7 142 us: sent_to_all(): return lax.all_to_all(copies, axis, split_axis=0, concat_axis=0, tiled=True)]
    dot_general x34 -> x0, matrix products: 52.6 us -> none  [highdot(): jnp.dot(left, right, precision=lax.Precision.HIGHEST, preferred_element_t...]
    psum x3 -> x0, blocking collectives: 48.2 us -> none  [by_axis(): return functools.reduce(lax.psum, axes, array)]
    all_to_all x3 -> x0, starting transfers between devices: 22.2 us -> none  [the longest x1 9.5 us: sum_in_two_steps(): lax.all_to_all(nearer, far, split_axis=0, concat_axis=0, tiled=True)]
    all_to_all x3 -> x0, waiting for transfers between devices: 12.2 us -> none  [the longest x1 5.77 us: sent_and_summed(): lax.all_to_all(in_blocks(array, dim, length), axis, 0, 0, tiled=True)]
    dot_general x17 -> x0, local copies, waits for them, and re-layouts: 7.19 us -> none  [highdot(): jnp.dot(left, right, precision=lax.Precision.HIGHEST, preferred_element_t...]
  transfers between devices with their start and end apart: 3 -> 0, of which waited for: 3 -> 0; matrix products, arithmetic and copies ran while one was open for 5% -> 0% of each run, Pallas kernels for 0% -> 0%
where the time goes in v1:
time: 207 us
  Pallas kernels  203 us (98%)
  local copies, waits for them, and re-layouts  3.33 us (2%)
    pallas_call x2, Pallas kernels, sum_over_rows(): pl.pallas_call(functools.partial(sum_kernel, total), in_specs=[VMEM], out...  66.8 us
    pallas_call x1, Pallas kernels, group_basis(): pl.pallas_call(functools.partial(basis_kernel, row_total), grid=(rows //...  43.3 us
    pallas_call x1, Pallas kernels, project(): pl.pallas_call(functools.partial(project_kernel, row_total), grid=(rows /...  40.2 us
    pallas_call x1, Pallas kernels, gathered(): pl.pallas_call(gather_kernel, in_specs=[VMEM], out_specs=VMEM, out_shape=...  36.4 us
    pallas_call x1, Pallas kernels, partial_gram(): pl.pallas_call(gram_kernel, grid=(rows // 896,), in_specs=[pl.BlockSpec((...  8.6 us
    pallas_call x1, Pallas kernels, partial_merge(): pl.pallas_call(merge_kernel, grid=(rows // 512,), in_specs=[pl.BlockSpec(...  7.87 us

profile of v1, /device:TPU:1, one launch (start us, length us, event | category | flops | bytes accessed | tf_op | source)
XLA Modules:
  0.0 206.5 jit_solution(3043136185614694430)
XLA Ops:
  0.0 1.6 copy.6.start_ref
  1.6 1.7 copy.5.start_ref
  3.3 8.6 %partial_gram.1.in_ref = f32[1536,128]{1,0:T(8,128)} custom-call(f32[3584,512]{1,0:T(8,128)} %x_ref.3), custom_call_target="tpu_custom_call" | custom-call | flops 3758096384 | bytes 7340032 | tf_op jit(solution)/shard_map/partial_gram/pallas_call | solution.py:136
  11.9 38.3 %sum_over_rows_0.1.gram_ref = f32[1536,128]{1,0:T(8,128)} custom-call(f32[1536,128]{1,0:T(8,128)} %partial_gram.1.in_ref), custom_call_target="tpu_custom_call" | custom-call | tf_op jit(solution)/shard_map/sum_over_rows_0/pallas_call | solution.py:219
  50.2 43.3 %group_basis.1.in_ref = f32[64,3584]{1,0:T(8,128)} custom-call(f32[1536,128]{1,0:T(8,128)} %sum_over_rows_0.1.gram_ref, f32[512,64]{1,0:T(8,128)} %copy.5.start_ref, f32[3584,512]{1,0:T(8,128)} %x_ref.3), custom_call_target="tpu_custom_call" | custom-call | tf_op jit(solution)/shard_map/group_basis/pallas_call | solution.py:257
  93.6 36.4 %gathered.1.joined_ref = f32[256,3584]{1,0:T(8,128)} custom-call(f32[64,3584]{1,0:T(8,128)} %group_basis.1.in_ref), custom_call_target="tpu_custom_call" | custom-call | tf_op jit(solution)/shard_map/gathered/pallas_call | solution.py:315
  130.0 7.9 %partial_merge.1.in_ref = f32[1024,128]{1,0:T(8,128)} custom-call(f32[256,3584]{1,0:T(8,128)} %gathered.1.joined_ref, f32[3584,128]{1,0:T(8,128)} %test_ref.1), custom_call_target="tpu_custom_call" | custom-call | tf_op jit(solution)/shard_map/partial_merge/pallas_call | solution.py:352
  137.8 28.5 %sum_over_rows_2.1.merge_ref = f32[1024,128]{1,0:T(8,128)} custom-call(f32[1024,128]{1,0:T(8,128)} %partial_merge.1.in_ref), custom_call_target="tpu_custom_call" | custom-call | tf_op jit(solution)/shard_map/sum_over_rows_2/pallas_call | solution.py:219
  166.3 40.2 %project.1 = f32[3584,128]{1,0:T(8,128)} custom-call(f32[1024,128]{1,0:T(8,128)} %sum_over_rows_2.1.merge_ref, f32[256,64]{1,0:T(8,128)} %copy.6.start_ref, f32[256,3584]{1,0:T(8,128)} %gathered.1.joined_ref), custom_call_target="tpu_custom_call" | custom-call | tf_op jit(solution)/shard_map/project/pallas_call | solution.py:386

commit v2 on v1

v2 whole, which is shorter than its diff:
```python
import functools

import jax
import jax.numpy as jnp
from jax import lax
from jax.experimental import pallas as pl
from jax.experimental.pallas import tpu as pltpu
from jax.sharding import Mesh
from jax.sharding import PartitionSpec as P

ITERS = 6
RANK = 64
ROW = ("row_0", "row_1", "row_2")
MESH = pl.DeviceIdType.MESH
F32, BF16 = jnp.float32, jnp.bfloat16
NT = (((1,), (1,)), ((), ()))
TN = (((0,), (0,)), ((), ()))
NN = (((1,), (0,)), ((), ()))
VMEM = pl.BlockSpec(memory_space=pltpu.VMEM)
GRAM_ROWS = 1536
MERGE_ROWS = 1024


def split(x):
    high = x.astype(BF16)
    return high, (x - high.astype(F32)).astype(BF16)


def bdot(a, b, dims):
    return lax.dot_general(a, b, dims, preferred_element_type=F32)


def fdot(a, b, dims=NN):
    return lax.dot_general(
        a, b, dims, precision=lax.Precision.HIGHEST, preferred_element_type=F32
    )


def lower_inverse(small):
    rows8 = lax.broadcasted_iota(jnp.int32, (8, 128), 0)
    row, lane = (lax.broadcasted_iota(jnp.int32, (64, 64), d) for d in (0, 1))
    joint = jnp.concatenate([jnp.where(row == lane, 1.0, 0.0), small], axis=1)
    bands = [joint[8 * k : 8 * k + 8, :] for k in range(8)]
    done, least, most = [], None, None
    for k in range(8):
        first = 64 + 8 * k
        cols = [
            [jnp.broadcast_to(bands[i][:, first + c : first + c + 1], (8, 128)) for c in range(8)]
            for i in range(k, 8)
        ]
        line = [jnp.broadcast_to(bands[k][a : a + 1, :], (8, 128)) for a in range(8)]
        piv = [[jnp.broadcast_to(cols[0][c][a : a + 1, :], (8, 128)) for c in range(a + 1)] for a in range(8)]
        inv, low = [None] * 8, [[None] * 8 for _ in range(8)]
        for a in range(8):
            inv[a] = 1.0 / piv[a][a]
            for c in range(a + 1, 8):
                low[c][a] = piv[c][a] * inv[a]
            for c in range(a + 1, 8):
                line[c] = line[c] - low[c][a] * line[a]
                for e in range(a + 1, c + 1):
                    piv[c][e] = piv[c][e] - low[c][a] * piv[e][a]
        band, diag = line[0], piv[0][0]
        for a in range(1, 8):
            band = jnp.where(rows8 == a, line[a], band)
            diag = jnp.where(rows8 == a, piv[a][a], diag)
        done.append(band * lax.rsqrt(diag))
        least = diag if least is None else jnp.minimum(least, diag)
        most = diag if most is None else jnp.maximum(most, diag)
        if k < 7:
            back = [line[a] * inv[a] for a in range(8)]
            for a in range(7, -1, -1):
                for c in range(a):
                    back[c] = back[c] - low[a][c] * back[a]
            for i in range(k + 1, 8):
                rest = bands[i]
                for a in range(8):
                    rest = rest - cols[i - k][a] * back[a]
                bands[i] = rest
    return jnp.concatenate(done, axis=0)[:, :64], jnp.min(least), jnp.max(most)


def split3(x):
    high = x.astype(BF16)
    rest = x - high.astype(F32)
    mid = rest.astype(BF16)
    return high, mid, (rest - mid.astype(F32)).astype(BF16)


def times(block, parts):
    three = jnp.concatenate(split3(block), axis=0)
    n = block.shape[0]
    one = bdot(three, parts[0], NN)
    two = bdot(three[: 2 * n], parts[1], NN)
    return one[:n] + ((one[n : 2 * n] + two[:n]) + (one[2 * n :] + two[n:]))


def orth_rows(block):
    inverse, least, most = lower_inverse(fdot(block, block, NT))
    return fdot(inverse, block), least / most


def sweeps(start, parts, out_ref, floor, last_floor):
    block, fine = start, None
    for pair in range(ITERS // 2):
        block, ratio = orth_rows(times(times(block, parts), parts))
        ok = ratio > (last_floor if pair == ITERS // 2 - 1 else floor)
        fine = ok if fine is None else jnp.logical_and(fine, ok)
    out_ref[...] = block

    @pl.when(jnp.logical_not(fine))
    def _():
        out_ref[...] = orth_rows(start)[0]

        def one(_, carry):
            out_ref[...] = orth_rows(times(out_ref[...], parts))[0]
            return carry

        lax.fori_loop(0, ITERS, one, 0)


def gram_kernel(x_ref, out_ref, first, second):
    step = pl.program_id(0)
    high, low = split(x_ref[...])
    one = bdot(high, high, TN)
    two = bdot(high, low, TN)

    @pl.when(step == 0)
    def _():
        first[...] = one
        second[...] = two

    @pl.when(step > 0)
    def _():
        first[...] = first[...] + one
        second[...] = second[...] + two

    @pl.when(step == pl.num_programs(0) - 1)
    def _():
        for at, (i, j) in enumerate(((0, 0), (0, 1), (1, 1))):
            block = (
                first[256 * i : 256 * i + 256, 256 * j : 256 * j + 256]
                + second[256 * i : 256 * i + 256, 256 * j : 256 * j + 256]
                + second[256 * j : 256 * j + 256, 256 * i : 256 * i + 256].T
            )
            for h in range(2):
                out_ref[512 * at + 256 * h : 512 * at + 256 * h + 256, :] = block[:, 128 * h : 128 * h + 128]


def partial_gram(snapshots):
    rows = snapshots.shape[0]
    return pl.pallas_call(
        gram_kernel,
        grid=(rows // 896,),
        in_specs=[pl.BlockSpec((896, 512), lambda i: (i, 0))],
        out_specs=pl.BlockSpec((GRAM_ROWS, 128), lambda i: (0, 0)),
        out_shape=jax.ShapeDtypeStruct((GRAM_ROWS, 128), F32),
        scratch_shapes=[pltpu.VMEM((512, 512), F32), pltpu.VMEM((512, 512), F32)],
        cost_estimate=pl.CostEstimate(flops=4 * rows * 512 * 512, bytes_accessed=rows * 2048, transcendentals=0),
        name="partial_gram",
    )(snapshots)


def rows_at(start, size):
    return pl.ds(pl.multiple_of(start, 8), size)


def remote(src, dst, send, recv, device):
    return pltpu.make_async_remote_copy(
        src_ref=src, dst_ref=dst, send_sem=send, recv_sem=recv, device_id=device, device_id_type=MESH
    )


def row_peers():
    grp = lax.axis_index("grp")
    y, z, c = (lax.axis_index(name) for name in ROW)
    along_y = [(lax.rem(y + d, 4), (grp, lax.rem(y + d, 4), z, c)) for d in range(1, 4)]
    along_z = [(lax.rem(z + d, 8), (grp, y, lax.rem(z + d, 8), c)) for d in range(1, 8)]
    return (grp, y, z, 1 - c), along_y, along_z


def greet(peers):
    barrier = pltpu.get_barrier_semaphore()
    for peer in peers:
        pl.semaphore_signal(barrier, inc=1, device_id=peer, device_id_type=MESH)
    pl.semaphore_wait(barrier, len(peers))


class StagedSum:
    def __init__(self, in_ref, out_ref, got1, sum1, got2, sum2, got3, send, recv):
        self.in_ref, self.out_ref = in_ref, out_ref
        self.got1, self.sum1, self.got2, self.sum2, self.got3 = got1, sum1, got2, sum2, got3
        self.send, self.recv = send, recv
        self.mate, self.along_y, self.along_z = row_peers()
        self.y, self.z, self.c = (lax.axis_index(name) for name in ROW)

    def copy(self, i, at, src, dst, device):
        return remote(src, dst, self.send.at[i, at], self.recv.at[i, at], device)

    def halves(self, i):
        src = self.in_ref.at[rows_at(512 * i + (1 - self.c) * 256, 256)]
        return [self.copy(i, 0, src, self.got1.at[i], self.mate)]

    def quarters(self, i):
        return [
            self.copy(i, 1 + d, self.sum1.at[i, rows_at(y * 64, 64)], self.got2.at[i, d], peer)
            for d, (y, peer) in enumerate(self.along_y)
        ]

    def eighths(self, i):
        return [
            self.copy(i, 4 + d, self.sum2.at[i, rows_at(z * 8, 8)], self.got3.at[i, d], peer)
            for d, (z, peer) in enumerate(self.along_z)
        ]

    def back_z(self, i):
        mine = self.out_ref.at[rows_at(512 * i + self.c * 256 + self.y * 64 + self.z * 8, 8)]
        return [self.copy(i, 11 + d, mine, mine, peer) for d, (_, peer) in enumerate(self.along_z)]

    def back_y(self, i):
        mine = self.out_ref.at[rows_at(512 * i + self.c * 256 + self.y * 64, 64)]
        return [self.copy(i, 18 + d, mine, mine, peer) for d, (_, peer) in enumerate(self.along_y)]

    def back_core(self, i):
        mine = self.out_ref.at[rows_at(512 * i + self.c * 256, 256)]
        return [self.copy(i, 21, mine, mine, self.mate)]

    def add(self, stage, i):
        if stage == 0:
            self.sum1[i] = self.in_ref[rows_at(512 * i + self.c * 256, 256), :] + self.got1[i]
        elif stage == 1:
            self.sum2[i] = self.sum1[i, rows_at(self.y * 64, 64), :] + self.got2[i, 0] + self.got2[i, 1] + self.got2[i, 2]
        elif stage == 2:
            total = self.sum2[i, rows_at(self.z * 8, 8), :]
            for d in range(7):
                total = total + self.got3[i, d]
            self.out_ref[rows_at(512 * i + self.c * 256 + self.y * 64 + self.z * 8, 8), :] = total

    def start(self, made):
        for one in made:
            one.start()
        return made

    def finish(self, flying):
        stages = [self.halves, self.quarters, self.eighths, self.back_z, self.back_y, self.back_core]
        for stage in range(6):
            for i in range(len(flying)):
                for one in flying[i]:
                    one.wait()
                self.add(stage, i)
                if stage < 5:
                    flying[i] = self.start(stages[stage + 1](i))


def sum_scratch(chunks):
    dma = pltpu.SemaphoreType.DMA
    return [
        pltpu.VMEM((chunks, 256, 128), F32),
        pltpu.VMEM((chunks, 256, 128), F32),
        pltpu.VMEM((chunks, 3, 64, 128), F32),
        pltpu.VMEM((chunks, 64, 128), F32),
        pltpu.VMEM((chunks, 7, 8, 128), F32),
        dma((chunks, 22)),
        dma((chunks, 22)),
    ]


def sum_kernel(in_ref, out_ref, *scratch):
    work = StagedSum(in_ref, out_ref, *scratch)
    greet([work.mate] + [peer for _, peer in work.along_y + work.along_z])
    work.finish([work.start(work.halves(i)) for i in range(in_ref.shape[0] // 512)])


def sum_over_rows(array, number):
    total = array.shape[0]
    return pl.pallas_call(
        sum_kernel,
        in_specs=[VMEM],
        out_specs=VMEM,
        out_shape=jax.ShapeDtypeStruct((total, 128), F32),
        scratch_shapes=sum_scratch(total // 512),
        compiler_params=pltpu.CompilerParams(collective_id=number, has_side_effects=True),
        name="sum_over_rows",
    )(array)


def basis_kernel(row_total, gram_ref, start_ref, x_ref, out_ref, gram, iterate, high_low):
    @pl.when(pl.program_id(0) == 0)
    def _():
        for at, (i, j) in enumerate(((0, 0), (0, 1), (1, 1))):
            for h in range(2):
                block = gram_ref[512 * at + 256 * h : 512 * at + 256 * h + 256, :] * (1.0 / row_total)
                gram[256 * i : 256 * i + 256, 256 * j + 128 * h : 256 * j + 128 * h + 128] = block
        gram[256:512, 0:256] = gram[0:256, 256:512].T
        sweeps(start_ref[...], split(gram[...]), iterate, 1e-5, 5e-4)
        high, low = split(iterate[...])
        high_low[0:RANK, :] = high
        high_low[RANK:, :] = low

    high, low = split(x_ref[...])
    both = bdot(high_low[...], high, NT)
    out_ref[...] = both[:RANK] + both[RANK:] + bdot(high_low[0:RANK, :], low, NT)


def group_basis(gram, start_block, snapshots, row_total):
    rows = snapshots.shape[0]
    return pl.pallas_call(
        functools.partial(basis_kernel, row_total),
        grid=(rows // 512,),
        in_specs=[
            pl.BlockSpec((GRAM_ROWS, 128), lambda i: (0, 0)),
            pl.BlockSpec((RANK, 512), lambda i: (0, 0)),
            pl.BlockSpec((512, 512), lambda i: (i, 0)),
        ],
        out_specs=pl.BlockSpec((RANK, 512), lambda i: (0, i)),
        out_shape=jax.ShapeDtypeStruct((RANK, rows), F32),
        scratch_shapes=[pltpu.VMEM((512, 512), F32), pltpu.VMEM((RANK, 512), F32), pltpu.VMEM((2 * RANK, 512), BF16)],
        name="group_basis",
    )(gram, start_block, snapshots)


def merge_products(q, joined_ref, test_ref, first, second, third):
    part = test_ref.shape[0] // 4
    high, low = split(joined_ref[:, q * part : (q + 1) * part])
    test_high, test_low = split(test_ref[q * part : (q + 1) * part, :])
    one = bdot(high, high, NT)
    two = bdot(high, low, NT)
    three = bdot(high, test_high, NN) + bdot(high, test_low, NN) + bdot(low, test_high, NN)
    if q == 0:
        first[...], second[...], third[...] = one, two, three
    else:
        first[...] = first[...] + one
        second[...] = second[...] + two
        third[...] = third[...] + three


def merge_kernel(in_ref, test_ref, out_ref, merge_ref, part_ref, first, second, third, send_g, recv_g, *scratch):
    g = lax.axis_index("grp")
    y, z, c = (lax.axis_index(name) for name in ROW)
    right, left = lax.rem(g + 1, 4), lax.rem(g + 3, 4)
    part = in_ref.shape[1] // 4
    work = StagedSum(part_ref, merge_ref, *scratch)
    greet([(right, y, z, c), (left, y, z, c), work.mate] + [peer for _, peer in work.along_y + work.along_z])

    def place(block, q, first_row, size):
        return out_ref.at[rows_at(block * RANK + first_row, size), pl.ds(q * part, part)]

    def own(q):
        src = in_ref.at[:, pl.ds(q * part, part)]
        return [
            remote(src, place(g, q, 0, RANK), send_g.at[k, q], recv_g.at[k, q], (peer, y, z, c))
            for k, peer in enumerate((right, left))
        ]

    def on(q):
        return [
            remote(place(block, q, at, 32), place(block, q, at, 32), send_g.at[k, q], recv_g.at[k, q], (peer, y, z, c))
            for k, block, at, peer in ((2, left, 0, right), (3, right, 32, left))
        ]

    owns, ons = [own(q) for q in range(4)], [on(q) for q in range(4)]

    def start(made):
        for one in made:
            one.start()

    def arrived(made):
        for one in made:
            one.wait_recv()

    start(owns[0])
    start(owns[1])
    out_ref[rows_at(g * RANK, RANK), :] = in_ref[...]
    for q in range(4):
        arrived(owns[q])
        start(ons[q])
        if q < 2:
            start(owns[q + 2])
        if q > 0:
            arrived(ons[q - 1])
            merge_products(q - 1, out_ref, test_ref, first, second, third)
    arrived(ons[3])
    merge_products(3, out_ref, test_ref, first, second, third)
    merged = first[...] + second[...] + second[...].T
    for h in range(2):
        part_ref[256 * h : 256 * h + 256, :] = merged[:, 128 * h : 128 * h + 128]
    part_ref[512:768, :] = third[...]
    part_ref[768:, :] = jnp.zeros((MERGE_ROWS - 768, 128), F32)
    work.finish([work.start(work.halves(i)) for i in range(MERGE_ROWS // 512)])
    for made in owns + ons:
        for one in made:
            one.wait_send()


def merged_over_rows(basis, test_block, number):
    rows = basis.shape[1]
    dma = pltpu.SemaphoreType.DMA
    return pl.pallas_call(
        merge_kernel,
        in_specs=[VMEM, VMEM],
        out_specs=[VMEM, VMEM],
        out_shape=[jax.ShapeDtypeStruct((4 * RANK, rows), F32), jax.ShapeDtypeStruct((MERGE_ROWS, 128), F32)],
        scratch_shapes=[
            pltpu.VMEM((MERGE_ROWS, 128), F32),
            pltpu.VMEM((256, 256), F32),
            pltpu.VMEM((256, 256), F32),
            pltpu.VMEM((256, 128), F32),
            dma((4, 4)),
            dma((4, 4)),
        ] + sum_scratch(MERGE_ROWS // 512),
        compiler_params=pltpu.CompilerParams(
            collective_id=number, has_side_effects=True, vmem_limit_bytes=48 * 1024 * 1024
        ),
        name="merged_over_rows",
    )(basis, test_block)


def project_kernel(row_total, merge_ref, start_ref, joined_ref, out_ref, merged, iterate, factor):
    @pl.when(pl.program_id(0) == 0)
    def _():
        for h in range(2):
            merged[:, 128 * h : 128 * h + 128] = merge_ref[256 * h : 256 * h + 256, :] * (1.0 / row_total)
        parts = split(merged[...])
        sweeps(start_ref[...], parts, iterate, 3e-6, 3e-6)
        coef = iterate[...]
        energy = fdot(times(coef, parts), coef, NT)
        coef = fdot(lower_inverse(energy)[0], coef)
        test_coeffs = fdot(coef, merge_ref[512:768, :]) * (1.0 / row_total)
        high, low = split(fdot(coef, test_coeffs, TN))
        factor[0] = high
        factor[1] = low

    high, low = split(joined_ref[...])
    out_ref[...] = bdot(high, factor[0], TN) + bdot(high, factor[1], TN) + bdot(low, factor[0], TN)


def project(merge, start_merge, joined, row_total):
    wide, rows = joined.shape
    return pl.pallas_call(
        functools.partial(project_kernel, row_total),
        grid=(rows // 512,),
        in_specs=[
            pl.BlockSpec((MERGE_ROWS, 128), lambda i: (0, 0)),
            pl.BlockSpec((RANK, 256), lambda i: (0, 0)),
            pl.BlockSpec((wide, 512), lambda i: (0, i)),
        ],
        out_specs=pl.BlockSpec((512, 128), lambda i: (i, 0)),
        out_shape=jax.ShapeDtypeStruct((rows, 128), F32),
        scratch_shapes=[pltpu.VMEM((256, 256), F32), pltpu.VMEM((RANK, 256), F32), pltpu.VMEM((2, 256, 128), BF16)],
        name="project",
    )(merge, start_merge, joined)


def on_device(snapshots, test_block, start_block, start_merge):
    row_total = snapshots.shape[0] * 64
    gram = sum_over_rows(partial_gram(snapshots), 0)
    basis = group_basis(gram, start_block.T, snapshots, row_total)
    joined, merge = merged_over_rows(basis, test_block, 1)
    return project(merge, start_merge.T, joined, row_total)


def solution(mesh):
    finer = Mesh(
        mesh.devices.reshape(mesh.shape["grp"], 4, 8, 2), ("grp", "row_0", "row_1", "row_2")
    )
    placed = (P(ROW, "grp"), P(ROW, "grp"), P("grp", None), P())
    return jax.shard_map(
        on_device, mesh=finer, in_specs=placed, out_specs=P(ROW, "grp"), check_vma=False
    )
```

time: 207 us -> 186 us (0.90)
  Pallas kernels: 203 us -> 183 us
    pallas_call x4 -> x2, Pallas kernels: 111 us -> 95.9 us  [the longest x1 60.6 us: merged_over_rows(): pl.pallas_call(merge_kernel, in_specs=[VMEM, VMEM], out_specs=[VMEM, VMEM...]
    pallas_call x1, Pallas kernels: 43.3 us -> 40 us  [group_basis(): pl.pallas_call(functools.partial(basis_kernel, row_total), grid=(rows //...]
where the time goes in v2:
time: 186 us; the launch traced here: 185 us
  Pallas kernels  183 us (98%)
  local copies, waits for them, and re-layouts  1.97 us (1%)
    pallas_call x1, Pallas kernels, merged_over_rows(): pl.pallas_call(merge_kernel, in_specs=[VMEM, VMEM], out_specs=[VMEM, VMEM...  60.6 us
    pallas_call x1, Pallas kernels, group_basis(): pl.pallas_call(functools.partial(basis_kernel, row_total), grid=(rows //...  40 us
    pallas_call x1, Pallas kernels, project(): pl.pallas_call(functools.partial(project_kernel, row_total), grid=(rows /...  38.7 us
    pallas_call x1, Pallas kernels, sum_over_rows(): pl.pallas_call(sum_kernel, in_specs=[VMEM], out_specs=VMEM, out_shape=jax...  35.3 us
    pallas_call x1, Pallas kernels, partial_gram(): pl.pallas_call(gram_kernel, grid=(rows // 896,), in_specs=[pl.BlockSpec((...  8.6 us

profile of v2, /device:TPU:1, one launch (start us, length us, event | category | flops | bytes accessed | tf_op | source)
XLA Modules:
  0.0 185.3 jit_solution(7569071475357501100)
XLA Ops:
  0.0 8.6 %partial_gram.1.in_ref = f32[1536,128]{1,0:T(8,128)} custom-call(f32[3584,512]{1,0:T(8,128)} %x_ref.3), custom_call_target="tpu_custom_call" | custom-call | flops 3758096384 | bytes 7340032 | tf_op jit(solution)/shard_map/partial_gram/pallas_call | solution.py:151
  8.6 35.3 %sum_over_rows.1.gram_ref = f32[1536,128]{1,0:T(8,128)} custom-call(f32[1536,128]{1,0:T(8,128)} %partial_gram.1.in_ref), custom_call_target="tpu_custom_call" | custom-call | tf_op jit(solution)/shard_map/sum_over_rows/pallas_call | solution.py:275
  43.9 0.0 copy-start.1
  43.9 40.0 %group_basis.1.in_ref = f32[64,3584]{1,0:T(8,128)} custom-call(f32[1536,128]{1,0:T(8,128)} %sum_over_rows.1.gram_ref, f32[64,512]{1,0:T(8,128)} %bitcast.2, f32[3584,512]{1,0:T(8,128)} %x_ref.3), custom_call_target="tpu_custom_call" | custom-call | tf_op jit(solution)/shard_map/group_basis/pallas_call | solution.py:306
  84.0 0.0 copy-done.1
  84.0 0.0 copy-start
  84.0 1.2 copy-done
  85.2 60.6 %merged_over_rows.1 = (f32[256,3584]{1,0:T(8,128)}, f32[1024,128]{1,0:T(8,128)S(1)}) custom-call(f32[64,3584]{1,0:T(8,128)S(1)} %copy-done, f32[3584,128]{1,0:T(8,128)S(1)} %copy-done.1), custom_call_target="tpu_custom_call" | custom-call | tf_op jit(solution)/shard_map/merged_over_rows/pallas_call | solution.py:397
  145.7 0.0 copy-start.2
  145.8 0.8 copy-done.2
  146.5 38.7 %project.1 = f32[3584,128]{1,0:T(8,128)} custom-call(f32[1024,128]{1,0:T(8,128)} %copy-done.2, f32[64,256]{1,0:T(8,128)} %bitcast.3, f32[256,3584]{1,0:T(8,128)} %get-tuple-element.8.joined_ref), custom_call_target="tpu_custom_call" | custom-call | tf_op jit(solution)/shard_map/project/pallas_call | solution.py:438
Async XLA Ops:
  43.9 40.1 %copy-start.1 = (f32[3584,128]{1,0:T(8,128)S(1)}, f32[3584,128]{1,0:T(8,128)}, u32[]{:S(2)}) copy-start(f32[3584,128]{1,0:T(8,128)} %test_ref.1) | copy-start | bytes 5505028
  84.0 1.2 copy-start
  145.7 0.8 copy-start.2

commit v3 on v2

--- a/solution.py
+++ b/solution.py
@@ -99,65 +99,21 @@
     return fdot(inverse, block), least / most
 
 
-def sweeps(start, parts, out_ref, floor, last_floor):
-    block, fine = start, None
-    for pair in range(ITERS // 2):
-        block, ratio = orth_rows(times(times(block, parts), parts))
-        ok = ratio > (last_floor if pair == ITERS // 2 - 1 else floor)
-        fine = ok if fine is None else jnp.logical_and(fine, ok)
-    out_ref[...] = block
-
-    @pl.when(jnp.logical_not(fine))
-    def _():
-        out_ref[...] = orth_rows(start)[0]
-
-        def one(_, carry):
-            out_ref[...] = orth_rows(times(out_ref[...], parts))[0]
-            return carry
-
-        lax.fori_loop(0, ITERS, one, 0)
-
-
-def gram_kernel(x_ref, out_ref, first, second):
-    step = pl.program_id(0)
-    high, low = split(x_ref[...])
-    one = bdot(high, high, TN)
-    two = bdot(high, low, TN)
-
-    @pl.when(step == 0)
-    def _():
-        first[...] = one
-        second[...] = two
-
-    @pl.when(step > 0)
-    def _():
-        first[...] = first[...] + one
-        second[...] = second[...] + two
-
-    @pl.when(step == pl.num_programs(0) - 1)
-    def _():
-        for at, (i, j) in enumerate(((0, 0), (0, 1), (1, 1))):
-            block = (
-                first[256 * i : 256 * i + 256, 256 * j : 256 * j + 256]
-                + second[256 * i : 256 * i + 256, 256 * j : 256 * j + 256]
-                + second[256 * j : 256 * j + 256, 256 * i : 256 * i + 256].T
-            )
-            for h in range(2):
-                out_ref[512 * at + 256 * h : 512 * at + 256 * h + 256, :] = block[:, 128 * h : 128 * h + 128]
-
-
-def partial_gram(snapshots):
-    rows = snapshots.shape[0]
-    return pl.pallas_call(
-        gram_kernel,
-        grid=(rows // 896,),
-        in_specs=[pl.BlockSpec((896, 512), lambda i: (i, 0))],
-        out_specs=pl.BlockSpec((GRAM_ROWS, 128), lambda i: (0, 0)),
-        out_shape=jax.ShapeDtypeStruct((GRAM_ROWS, 128), F32),
-        scratch_shapes=[pltpu.VMEM((512, 512), F32), pltpu.VMEM((512, 512), F32)],
-        cost_estimate=pl.CostEstimate(flops=4 * rows * 512 * 512, bytes_accessed=rows * 2048, transcendentals=0),
-        name="partial_gram",
-    )(snapshots)
+def corrected(block, images):
+    row, lane = (lax.broadcasted_iota(jnp.int32, (RANK, RANK), d) for d in (0, 1))
+    excess = fdot(block, images, NT) - jnp.where(row == lane, 1.0, 0.0)
+    part = jnp.where(row > lane, excess, jnp.where(row == lane, 0.5 * excess, 0.0))
+    return block - fdot(part, block), jnp.sum(excess * excess)
+
+
+def step_by_step(start, parts, out_ref):
+    out_ref[...] = orth_rows(start)[0]
+
+    def one(_, carry):
+        out_ref[...] = orth_rows(times(out_ref[...], parts))[0]
+        return carry
+
+    lax.fori_loop(0, ITERS, one, 0)
 
 
 def rows_at(start, size):
@@ -182,7 +138,20 @@
     barrier = pltpu.get_barrier_semaphore()
     for peer in peers:
         pl.semaphore_signal(barrier, inc=1, device_id=peer, device_id_type=MESH)
-    pl.semaphore_wait(barrier, len(peers))
+
+
+def meet(peers):
+    pl.semaphore_wait(pltpu.get_barrier_semaphore(), len(peers))
+
+
+def pieces_in(src, dst, sem):
+    part = src.shape[0] // 4
+    made = [
+        pltpu.make_async_copy(src.at[pl.ds(q * part, part)], dst.at[pl.ds(q * part, part)], sem.at[q]) for q in range(4)
+    ]
+    for one in made:
+        one.start()
+    return made
 
 
 class StagedSum:
@@ -190,6 +159,7 @@
         self.in_ref, self.out_ref = in_ref, out_ref
         self.got1, self.sum1, self.got2, self.sum2, self.got3 = got1, sum1, got2, sum2, got3
         self.send, self.recv = send, recv
+        self.stage, self.flying = {}, {}
         self.mate, self.along_y, self.along_z = row_peers()
         self.y, self.z, self.c = (lax.axis_index(name) for name in ROW)
 
@@ -235,20 +205,29 @@
                 total = total + self.got3[i, d]
             self.out_ref[rows_at(512 * i + self.c * 256 + self.y * 64 + self.z * 8, 8), :] = total
 
-    def start(self, made):
-        for one in made:
+    def begin(self, i):
+        self.stage[i], self.flying[i] = 0, self.halves(i)
+        for one in self.flying[i]:
             one.start()
-        return made
-
-    def finish(self, flying):
-        stages = [self.halves, self.quarters, self.eighths, self.back_z, self.back_y, self.back_core]
-        for stage in range(6):
-            for i in range(len(flying)):
-                for one in flying[i]:
-                    one.wait()
-                self.add(stage, i)
-                if stage < 5:
-                    flying[i] = self.start(stages[stage + 1](i))
+
+    def advance(self, i):
+        for one in self.flying[i]:
+            one.wait()
+        stage = self.stage[i]
+        self.add(stage, i)
+        self.stage[i] = stage + 1
+        if stage < 5:
+            following = (self.quarters, self.eighths, self.back_z, self.back_y, self.back_core)[stage]
+            self.flying[i] = following(i)
+            for one in self.flying[i]:
+                one.start()
+
+    def finish(self):
+        while min(self.stage.values()) < 6:
+            low = min(self.stage.values())
+            for i in sorted(self.stage):
+                if self.stage[i] == low:
+                    self.advance(i)
 
 
 def sum_scratch(chunks):
@@ -264,58 +243,100 @@
     ]
 
 
-def sum_kernel(in_ref, out_ref, *scratch):
-    work = StagedSum(in_ref, out_ref, *scratch)
-    greet([work.mate] + [peer for _, peer in work.along_y + work.along_z])
-    work.finish([work.start(work.halves(i)) for i in range(in_ref.shape[0] // 512)])
-
-
-def sum_over_rows(array, number):
-    total = array.shape[0]
-    return pl.pallas_call(
-        sum_kernel,
-        in_specs=[VMEM],
-        out_specs=VMEM,
-        out_shape=jax.ShapeDtypeStruct((total, 128), F32),
-        scratch_shapes=sum_scratch(total // 512),
-        compiler_params=pltpu.CompilerParams(collective_id=number, has_side_effects=True),
-        name="sum_over_rows",
-    )(array)
-
-
-def basis_kernel(row_total, gram_ref, start_ref, x_ref, out_ref, gram, iterate, high_low):
-    @pl.when(pl.program_id(0) == 0)
-    def _():
-        for at, (i, j) in enumerate(((0, 0), (0, 1), (1, 1))):
-            for h in range(2):
-                block = gram_ref[512 * at + 256 * h : 512 * at + 256 * h + 256, :] * (1.0 / row_total)
-                gram[256 * i : 256 * i + 256, 256 * j + 128 * h : 256 * j + 128 * h + 128] = block
-        gram[256:512, 0:256] = gram[0:256, 256:512].T
-        sweeps(start_ref[...], split(gram[...]), iterate, 1e-5, 5e-4)
-        high, low = split(iterate[...])
-        high_low[0:RANK, :] = high
-        high_low[RANK:, :] = low
-
-    high, low = split(x_ref[...])
-    both = bdot(high_low[...], high, NT)
-    out_ref[...] = both[:RANK] + both[RANK:] + bdot(high_low[0:RANK, :], low, NT)
-
-
-def group_basis(gram, start_block, snapshots, row_total):
+def pack(at, block, out_ref):
+    for h in range(2):
+        out_ref[512 * at + 256 * h : 512 * at + 256 * h + 256, :] = block[:, 128 * h : 128 * h + 128]
+
+
+def gram_first(x_pieces, x_ref, high_ref, low_ref, out_ref):
+    part = x_ref.shape[0] // 4
+    one = two = None
+    for q in range(4):
+        x_pieces[q].wait()
+        here = slice(q * part, q * part + part)
+        high, low = split(x_ref[here, :])
+        high_ref[here, :], low_ref[here, :] = high, low
+        a, b = bdot(high[:, :256], high[:, :256], TN), bdot(high[:, :256], low[:, :256], TN)
+        one, two = (a, b) if one is None else (one + a, two + b)
+    pack(0, one + two + two.T, out_ref)
+
+
+def gram_second(high_ref, low_ref, out_ref):
+    left, right = high_ref[:, :256], high_ref[:, 256:]
+    pack(1, bdot(left, right, TN) + bdot(left, low_ref[:, 256:], TN) + bdot(low_ref[:, :256], right, TN), out_ref)
+
+
+def gram_third(high_ref, low_ref, out_ref):
+    both = bdot(high_ref[:, 256:], jnp.concatenate([high_ref[:, 256:], low_ref[:, 256:]], axis=1), TN)
+    pack(2, both[:, :256] + both[:, 256:] + both[:, 256:].T, out_ref)
+
+
+def gram_kernel(x_hbm, out_ref, x_ref, high_ref, low_ref, part_ref, x_sem, *scratch):
+    work = StagedSum(part_ref, out_ref, *scratch)
+    peers = [work.mate] + [peer for _, peer in work.along_y + work.along_z]
+    x_pieces = pieces_in(x_hbm, x_ref, x_sem)
+    greet(peers)
+    gram_first(x_pieces, x_ref, high_ref, low_ref, part_ref)
+    meet(peers)
+    work.begin(0)
+    gram_second(high_ref, low_ref, part_ref)
+    work.begin(1)
+    work.advance(0)
+    gram_third(high_ref, low_ref, part_ref)
+    work.begin(2)
+    work.advance(1)
+    work.advance(0)
+    work.finish()
+
+
+def gram_over_rows(snapshots, number):
     rows = snapshots.shape[0]
     return pl.pallas_call(
-        functools.partial(basis_kernel, row_total),
-        grid=(rows // 512,),
-        in_specs=[
-            pl.BlockSpec((GRAM_ROWS, 128), lambda i: (0, 0)),
-            pl.BlockSpec((RANK, 512), lambda i: (0, 0)),
-            pl.BlockSpec((512, 512), lambda i: (i, 0)),
-        ],
-        out_specs=pl.BlockSpec((RANK, 512), lambda i: (0, i)),
-        out_shape=jax.ShapeDtypeStruct((RANK, rows), F32),
-        scratch_shapes=[pltpu.VMEM((512, 512), F32), pltpu.VMEM((RANK, 512), F32), pltpu.VMEM((2 * RANK, 512), BF16)],
-        name="group_basis",
-    )(gram, start_block, snapshots)
+        gram_kernel,
+        in_specs=[pl.BlockSpec(memory_space=pl.ANY)],
+        out_specs=VMEM,
+        out_shape=jax.ShapeDtypeStruct((GRAM_ROWS, 128), F32),
+        scratch_shapes=[
+            pltpu.VMEM((rows, 512), F32),
+            pltpu.VMEM((rows, 512), BF16),
+            pltpu.VMEM((rows, 512), BF16),
+            pltpu.VMEM((GRAM_ROWS, 128), F32),
+            pltpu.SemaphoreType.DMA((4,)),
+        ] + sum_scratch(GRAM_ROWS // 512),
+        compiler_params=pltpu.CompilerParams(
+            collective_id=number, has_side_effects=True, vmem_limit_bytes=48 * 1024 * 1024
+        ),
+        name="gram_over_rows",
+    )(snapshots)
+
+
+def solve_kernel(row_total, gram_ref, start_ref, out_ref, gram):
+    for at, (i, j) in enumerate(((0, 0), (0, 1), (1, 1))):
+        for h in range(2):
+            block = gram_ref[512 * at + 256 * h : 512 * at + 256 * h + 256, :] * (1.0 / row_total)
+            gram[256 * i : 256 * i + 256, 256 * j + 128 * h : 256 * j + 128 * h + 128] = block
+    gram[256:512, 0:256] = gram[0:256, 256:512].T
+    parts = split(gram[...])
+    block, ratio = orth_rows(times(times(times(start_ref[...], parts), parts), parts))
+    block, last_ratio = orth_rows(times(times(times(block, parts), parts), parts))
+    block, error = corrected(block, block)
+    out_ref[...] = block
+    fine = jnp.logical_and(jnp.minimum(ratio, last_ratio) > 3e-6, error < 1e-5)
+
+    @pl.when(jnp.logical_not(fine))
+    def _():
+        step_by_step(start_ref[...], parts, out_ref)
+
+
+def group_solve(gram, start_block, row_total):
+    return pl.pallas_call(
+        functools.partial(solve_kernel, row_total),
+        in_specs=[VMEM, VMEM],
+        out_specs=VMEM,
+        out_shape=jax.ShapeDtypeStruct((RANK, 512), F32),
+        scratch_shapes=[pltpu.VMEM((512, 512), F32)],
+        name="group_solve",
+    )(gram, start_block)
 
 
 def merge_products(q, joined_ref, test_ref, first, second, third):
@@ -333,21 +354,31 @@
         third[...] = third[...] + three
 
 
-def merge_kernel(in_ref, test_ref, out_ref, merge_ref, part_ref, first, second, third, send_g, recv_g, *scratch):
+def basis_piece(high_low, x):
+    high, low = split(x)
+    both = bdot(high_low, high, NT)
+    return both[:RANK] + both[RANK:] + bdot(high_low[:RANK], low, NT)
+
+
+def merge_kernel(
+    iterate_ref, x_hbm, test_ref, out_ref, merge_ref, x_ref, part_ref, first, second, third, x_sem, send_g, recv_g, *scratch
+):
     g = lax.axis_index("grp")
     y, z, c = (lax.axis_index(name) for name in ROW)
     right, left = lax.rem(g + 1, 4), lax.rem(g + 3, 4)
-    part = in_ref.shape[1] // 4
+    part = x_ref.shape[0] // 4
+    x_pieces = pieces_in(x_hbm, x_ref, x_sem)
     work = StagedSum(part_ref, merge_ref, *scratch)
-    greet([(right, y, z, c), (left, y, z, c), work.mate] + [peer for _, peer in work.along_y + work.along_z])
+    peers = [(right, y, z, c), (left, y, z, c), work.mate] + [peer for _, peer in work.along_y + work.along_z]
+    greet(peers)
+    high_low = jnp.concatenate(split(iterate_ref[...]), axis=0)
 
     def place(block, q, first_row, size):
         return out_ref.at[rows_at(block * RANK + first_row, size), pl.ds(q * part, part)]
 
     def own(q):
-        src = in_ref.at[:, pl.ds(q * part, part)]
         return [
-            remote(src, place(g, q, 0, RANK), send_g.at[k, q], recv_g.at[k, q], (peer, y, z, c))
+            remote(place(g, q, 0, RANK), place(g, q, 0, RANK), send_g.at[k, q], recv_g.at[k, q], (peer, y, z, c))
             for k, peer in enumerate((right, left))
         ]
 
@@ -367,15 +398,26 @@
         for one in made:
             one.wait_recv()
 
+    def make(q):
+        x_pieces[q].wait()
+        out_ref[rows_at(g * RANK, RANK), q * part : (q + 1) * part] = basis_piece(
+            high_low, x_ref[q * part : (q + 1) * part, :]
+        )
+
+    make(0)
+    meet(peers)
     start(owns[0])
+    make(1)
     start(owns[1])
-    out_ref[rows_at(g * RANK, RANK), :] = in_ref[...]
+    make(2)
     for q in range(4):
         arrived(owns[q])
         start(ons[q])
         if q < 2:
             start(owns[q + 2])
-        if q > 0:
+        if q == 0:
+            make(3)
+        else:
             arrived(ons[q - 1])
             merge_products(q - 1, out_ref, test_ref, first, second, third)
     arrived(ons[3])
@@ -383,27 +425,31 @@
     merged = first[...] + second[...] + second[...].T
     for h in range(2):
         part_ref[256 * h : 256 * h + 256, :] = merged[:, 128 * h : 128 * h + 128]
+    work.begin(0)
     part_ref[512:768, :] = third[...]
     part_ref[768:, :] = jnp.zeros((MERGE_ROWS - 768, 128), F32)
-    work.finish([work.start(work.halves(i)) for i in range(MERGE_ROWS // 512)])
+    work.begin(1)
+    work.finish()
     for made in owns + ons:
         for one in made:
             one.wait_send()
 
 
-def merged_over_rows(basis, test_block, number):
-    rows = basis.shape[1]
+def merged_over_rows(iterate, snapshots, test_block, number):
+    rows = snapshots.shape[0]
     dma = pltpu.SemaphoreType.DMA
     return pl.pallas_call(
         merge_kernel,
-        in_specs=[VMEM, VMEM],
+        in_specs=[VMEM, pl.BlockSpec(memory_space=pl.ANY), VMEM],
         out_specs=[VMEM, VMEM],
         out_shape=[jax.ShapeDtypeStruct((4 * RANK, rows), F32), jax.ShapeDtypeStruct((MERGE_ROWS, 128), F32)],
         scratch_shapes=[
+            pltpu.VMEM((rows, 512), F32),
             pltpu.VMEM((MERGE_ROWS, 128), F32),
             pltpu.VMEM((256, 256), F32),
             pltpu.VMEM((256, 256), F32),
             pltpu.VMEM((256, 128), F32),
+            dma((4,)),
             dma((4, 4)),
             dma((4, 4)),
         ] + sum_scratch(MERGE_ROWS // 512),
@@ -411,26 +457,41 @@
             collective_id=number, has_side_effects=True, vmem_limit_bytes=48 * 1024 * 1024
         ),
         name="merged_over_rows",
-    )(basis, test_block)
-
-
-def project_kernel(row_total, merge_ref, start_ref, joined_ref, out_ref, merged, iterate, factor):
+    )(iterate, snapshots, test_block)
+
+
+def project_kernel(row_total, merge_ref, start_ref, joined_ref, out_ref, merged, coef_ref, factor):
     @pl.when(pl.program_id(0) == 0)
     def _():
         for h in range(2):
             merged[:, 128 * h : 128 * h + 128] = merge_ref[256 * h : 256 * h + 256, :] * (1.0 / row_total)
         parts = split(merged[...])
-        sweeps(start_ref[...], parts, iterate, 3e-6, 3e-6)
-        coef = iterate[...]
-        energy = fdot(times(coef, parts), coef, NT)
-        coef = fdot(lower_inverse(energy)[0], coef)
+
+        def to_modes(block):
+            inverse, _, _ = lower_inverse(fdot(times(block, parts), block, NT))
+            block = fdot(inverse, block)
+            return corrected(block, times(block, parts))
+
+        block, ratio = orth_rows(times(times(start_ref[...], parts), parts))
+        block, next_ratio = orth_rows(times(times(block, parts), parts))
+        coef, error = to_modes(times(times(block, parts), parts))
+        coef_ref[...] = coef
+        fine = jnp.logical_and(jnp.minimum(ratio, next_ratio) > 3e-6, error < 1e-4)
+
+        @pl.when(jnp.logical_not(fine))
+        def _():
+            step_by_step(start_ref[...], parts, coef_ref)
+            coef_ref[...] = to_modes(coef_ref[...])[0]
+
+        coef = coef_ref[...]
         test_coeffs = fdot(coef, merge_ref[512:768, :]) * (1.0 / row_total)
-        high, low = split(fdot(coef, test_coeffs, TN))
-        factor[0] = high
-        factor[1] = low
+        high, low = split(fdot(test_coeffs, coef, TN))
+        factor[0:128, :] = high
+        factor[128:, :] = low
 
     high, low = split(joined_ref[...])
-    out_ref[...] = bdot(high, factor[0], TN) + bdot(high, factor[1], TN) + bdot(low, factor[0], TN)
+    both = bdot(factor[...], high, NN)
+    out_ref[...] = (both[:128] + both[128:] + bdot(factor[0:128, :], low, NN)).T
 
 
 def project(merge, start_merge, joined, row_total):
@@ -445,16 +506,16 @@
         ],
         out_specs=pl.BlockSpec((512, 128), lambda i: (i, 0)),
         out_shape=jax.ShapeDtypeStruct((rows, 128), F32),
-        scratch_shapes=[pltpu.VMEM((256, 256), F32), pltpu.VMEM((RANK, 256), F32), pltpu.VMEM((2, 256, 128), BF16)],
+        scratch_shapes=[pltpu.VMEM((256, 256), F32), pltpu.VMEM((RANK, 256), F32), pltpu.VMEM((256, 256), BF16)],
         name="project",
     )(merge, start_merge, joined)
 
 
 def on_device(snapshots, test_block, start_block, start_merge):
     row_total = snapshots.shape[0] * 64
-    gram = sum_over_rows(partial_gram(snapshots), 0)
-    basis = group_basis(gram, start_block.T, snapshots, row_total)
-    joined, merge = merged_over_rows(basis, test_block, 1)
+    gram = gram_over_rows(snapshots, 0)
+    iterate = group_solve(gram, start_block.T, row_total)
+    joined, merge = merged_over_rows(iterate, snapshots, test_block, 1)
     return project(merge, start_merge.T, joined, row_total)
 
 

time: 186 us -> 177 us (0.952)
  Pallas kernels: 183 us -> 173 us
  local copies, waits for them, and re-layouts: 1.97 us -> 4.37 us
    pallas_call x4 -> x3, Pallas kernels: 145 us -> 133 us  [the longest x1 60.7 us: merged_over_rows(): pl.pallas_call(merge_kernel, in_specs=[VMEM, pl.BlockSpec(memory_space=pl...]
    unnamed x6 -> x10, local copies, waits for them, and re-layouts: 1.97 us -> 4.37 us
where the time goes in v3:
time: 177 us
  Pallas kernels  173 us (98%)
  local copies, waits for them, and re-layouts  4.37 us (2%)
    pallas_call x1, Pallas kernels, merged_over_rows(): pl.pallas_call(merge_kernel, in_specs=[VMEM, pl.BlockSpec(memory_space=pl...  60.7 us
    pallas_call x1, Pallas kernels, gram_over_rows(): pl.pallas_call(gram_kernel, in_specs=[pl.BlockSpec(memory_space=pl.ANY)],...  40.5 us
    pallas_call x1, Pallas kernels, project(): pl.pallas_call(functools.partial(project_kernel, row_total), grid=(rows /...  39.9 us
    pallas_call x1, Pallas kernels, group_solve(): pl.pallas_call(functools.partial(solve_kernel, row_total), in_specs=[VMEM...  31.6 us
    unnamed x10, local copies, waits for them, and re-layouts  4.37 us

profile of v3, /device:TPU:1, one launch (start us, length us, event | category | flops | bytes accessed | tf_op | source)
XLA Modules:
  0.0 177.1 jit_solution(4578131164987102192)
XLA Ops:
  0.0 0.0 copy-start.2
  0.0 40.5 %gram_over_rows.1.gram_ref = f32[1536,128]{1,0:T(8,128)S(1)} custom-call(f32[3584,512]{1,0:T(8,128)} %x_hbm.3), custom_call_target="tpu_custom_call" | custom-call | tf_op jit(solution)/shard_map/gram_over_rows/pallas_call | solution.py:294
  40.5 0.0 copy-start.1
  40.5 0.9 copy-done.1
  41.4 31.6 %group_solve.1.iterate_ref = f32[64,512]{1,0:T(8,128)} custom-call(f32[1536,128]{1,0:T(8,128)} %copy-done.1, f32[64,512]{1,0:T(8,128)} %bitcast.2), custom_call_target="tpu_custom_call" | custom-call | tf_op jit(solution)/shard_map/group_solve/pallas_call | solution.py:332
  73.0 0.0 copy-done.2
  73.0 0.0 copy-start.3
  73.0 0.9 copy-done.3
  73.9 60.7 %merged_over_rows.1 = (f32[256,3584]{1,0:T(8,128)S(1)}, f32[1024,128]{1,0:T(8,128)S(1)}) custom-call(f32[64,512]{1,0:T(8,128)S(1)} %copy-done.3, f32[3584,512]{1,0:T(8,128)} %x_hbm.3, f32[3584,128]{1,0:T(8,128)S(1)} %copy-done.2), custom_call_target="tpu_custom_call" | custom-call | tf_op jit(solution)/shard_map/merged_over_rows/pallas_call | solution.py:441
  134.6 0.0 copy-start
  134.6 1.8 %copy-done = f32[256,3584]{1,0:T(8,128)} copy-done((f32[256,3584]{1,0:T(8,128)}, f32[256,3584]{1,0:T(8,128)S(1)}, u32[]{:S(2)}) %copy-start) | copy-done | bytes 3670040
  136.4 0.0 copy-start.4
  136.4 0.8 copy-done.4
  137.2 39.9 %project.1 = f32[3584,128]{1,0:T(8,128)} custom-call(f32[1024,128]{1,0:T(8,128)} %copy-done.4, f32[64,256]{1,0:T(8,128)} %bitcast.3, f32[256,3584]{1,0:T(8,128)} %copy-done), custom_call_target="tpu_custom_call" | custom-call | tf_op jit(solution)/shard_map/project/pallas_call | solution.py:499
Async XLA Ops:
  0.0 73.0 %copy-start.2 = (f32[3584,128]{1,0:T(8,128)S(1)}, f32[3584,128]{1,0:T(8,128)}, u32[]{:S(2)}) copy-start(f32[3584,128]{1,0:T(8,128)} %test_ref.1) | copy-start | bytes 5505028
  40.5 0.9 copy-start.1
  73.0 0.9 copy-start.3
  134.6 1.8 %copy-start = (f32[256,3584]{1,0:T(8,128)}, f32[256,3584]{1,0:T(8,128)S(1)}, u32[]{:S(2)}) copy-start(f32[256,3584]{1,0:T(8,128)S(1)} %get-tuple-element.8.joined_ref) | copy-start | bytes 11010052
  136.4 0.8 copy-start.4

commit v4 on v3

--- a/solution.py
+++ b/solution.py
@@ -36,6 +36,10 @@
     )
 
 
+def spread(x):
+    return jnp.broadcast_to(x, (8, 128))
+
+
 def lower_inverse(small):
     rows8 = lax.broadcasted_iota(jnp.int32, (8, 128), 0)
     row, lane = (lax.broadcasted_iota(jnp.int32, (64, 64), d) for d in (0, 1))
@@ -44,21 +48,22 @@
     done, least, most = [], None, None
     for k in range(8):
         first = 64 + 8 * k
-        cols = [
-            [jnp.broadcast_to(bands[i][:, first + c : first + c + 1], (8, 128)) for c in range(8)]
-            for i in range(k, 8)
-        ]
-        line = [jnp.broadcast_to(bands[k][a : a + 1, :], (8, 128)) for a in range(8)]
-        piv = [[jnp.broadcast_to(cols[0][c][a : a + 1, :], (8, 128)) for c in range(a + 1)] for a in range(8)]
-        inv, low = [None] * 8, [[None] * 8 for _ in range(8)]
+        cols = [[spread(bands[i][:, first + c : first + c + 1]) for c in range(8)] for i in range(k, 8)]
+        line = [spread(bands[k][a : a + 1, :]) for a in range(8)]
+        piv = [[spread(cols[0][c][a : a + 1, :]) for c in range(a + 1)] for a in range(8)]
         for a in range(8):
-            inv[a] = 1.0 / piv[a][a]
+            inv = 1.0 / piv[a][a]
+            low = {c: piv[c][a] * inv for c in range(a + 1, 8)}
             for c in range(a + 1, 8):
-                low[c][a] = piv[c][a] * inv[a]
+                for e in range(a + 1, c + 1):
+                    piv[c][e] = piv[c][e] - low[c] * piv[e][a]
             for c in range(a + 1, 8):
-                line[c] = line[c] - low[c][a] * line[a]
-                for e in range(a + 1, c + 1):
-                    piv[c][e] = piv[c][e] - low[c][a] * piv[e][a]
+                line[c] = line[c] - low[c] * line[a]
+            for i in range(1, 8 - k):
+                share = cols[i][a] * inv
+                bands[k + i] = bands[k + i] - share * line[a]
+                for c in range(a + 1, 8):
+                    cols[i][c] = cols[i][c] - share * piv[c][a]
         band, diag = line[0], piv[0][0]
         for a in range(1, 8):
             band = jnp.where(rows8 == a, line[a], band)
@@ -66,16 +71,6 @@
         done.append(band * lax.rsqrt(diag))
         least = diag if least is None else jnp.minimum(least, diag)
         most = diag if most is None else jnp.maximum(most, diag)
-        if k < 7:
-            back = [line[a] * inv[a] for a in range(8)]
-            for a in range(7, -1, -1):
-                for c in range(a):
-                    back[c] = back[c] - low[a][c] * back[a]
-            for i in range(k + 1, 8):
-                rest = bands[i]
-                for a in range(8):
-                    rest = rest - cols[i - k][a] * back[a]
-                bands[i] = rest
     return jnp.concatenate(done, axis=0)[:, :64], jnp.min(least), jnp.max(most)
 
 
@@ -91,7 +86,8 @@
     n = block.shape[0]
     one = bdot(three, parts[0], NN)
     two = bdot(three[: 2 * n], parts[1], NN)
-    return one[:n] + ((one[n : 2 * n] + two[:n]) + (one[2 * n :] + two[n:]))
+    low = one[2 * n :] + two[n:] + bdot(three[:n], parts[2], NN)
+    return one[:n] + ((one[n : 2 * n] + two[:n]) + low)
 
 
 def orth_rows(block):
@@ -145,9 +141,11 @@
 
 
 def pieces_in(src, dst, sem):
-    part = src.shape[0] // 4
+    count = sem.shape[0]
+    part = src.shape[0] // count
     made = [
-        pltpu.make_async_copy(src.at[pl.ds(q * part, part)], dst.at[pl.ds(q * part, part)], sem.at[q]) for q in range(4)
+        pltpu.make_async_copy(src.at[pl.ds(q * part, part)], dst.at[pl.ds(q * part, part)], sem.at[q])
+        for q in range(count)
     ]
     for one in made:
         one.start()
@@ -316,7 +314,7 @@
             block = gram_ref[512 * at + 256 * h : 512 * at + 256 * h + 256, :] * (1.0 / row_total)
             gram[256 * i : 256 * i + 256, 256 * j + 128 * h : 256 * j + 128 * h + 128] = block
     gram[256:512, 0:256] = gram[0:256, 256:512].T
-    parts = split(gram[...])
+    parts = split3(gram[...])
     block, ratio = orth_rows(times(times(times(start_ref[...], parts), parts), parts))
     block, last_ratio = orth_rows(times(times(times(block, parts), parts), parts))
     block, error = corrected(block, block)
@@ -335,12 +333,16 @@
         out_specs=VMEM,
         out_shape=jax.ShapeDtypeStruct((RANK, 512), F32),
         scratch_shapes=[pltpu.VMEM((512, 512), F32)],
+        compiler_params=pltpu.CompilerParams(vmem_limit_bytes=16 * 1024 * 1024),
         name="group_solve",
     )(gram, start_block)
 
 
+PIECES = 7
+
+
 def merge_products(q, joined_ref, test_ref, first, second, third):
-    part = test_ref.shape[0] // 4
+    part = test_ref.shape[0] // PIECES
     high, low = split(joined_ref[:, q * part : (q + 1) * part])
     test_high, test_low = split(test_ref[q * part : (q + 1) * part, :])
     one = bdot(high, high, NT)
@@ -366,7 +368,7 @@
     g = lax.axis_index("grp")
     y, z, c = (lax.axis_index(name) for name in ROW)
     right, left = lax.rem(g + 1, 4), lax.rem(g + 3, 4)
-    part = x_ref.shape[0] // 4
+    part = x_ref.shape[0] // PIECES
     x_pieces = pieces_in(x_hbm, x_ref, x_sem)
     work = StagedSum(part_ref, merge_ref, *scratch)
     peers = [(right, y, z, c), (left, y, z, c), work.mate] + [peer for _, peer in work.along_y + work.along_z]
@@ -388,7 +390,7 @@
             for k, block, at, peer in ((2, left, 0, right), (3, right, 32, left))
         ]
 
-    owns, ons = [own(q) for q in range(4)], [on(q) for q in range(4)]
+    owns, ons = [own(q) for q in range(PIECES)], [on(q) for q in range(PIECES)]
 
     def start(made):
         for one in made:
@@ -410,18 +412,18 @@
     make(1)
     start(owns[1])
     make(2)
-    for q in range(4):
+    for q in range(PIECES):
         arrived(owns[q])
         start(ons[q])
-        if q < 2:
+        if q + 2 < PIECES:
             start(owns[q + 2])
-        if q == 0:
-            make(3)
-        else:
+        if q + 3 < PIECES:
+            make(q + 3)
+        if q > 0:
             arrived(ons[q - 1])
             merge_products(q - 1, out_ref, test_ref, first, second, third)
-    arrived(ons[3])
-    merge_products(3, out_ref, test_ref, first, second, third)
+    arrived(ons[PIECES - 1])
+    merge_products(PIECES - 1, out_ref, test_ref, first, second, third)
     merged = first[...] + second[...] + second[...].T
     for h in range(2):
         part_ref[256 * h : 256 * h + 256, :] = merged[:, 128 * h : 128 * h + 128]
@@ -449,9 +451,9 @@
             pltpu.VMEM((256, 256), F32),
             pltpu.VMEM((256, 256), F32),
             pltpu.VMEM((256, 128), F32),
-            dma((4,)),
-            dma((4, 4)),
-            dma((4, 4)),
+            dma((PIECES,)),
+            dma((4, PIECES)),
+            dma((4, PIECES)),
         ] + sum_scratch(MERGE_ROWS // 512),
         compiler_params=pltpu.CompilerParams(
             collective_id=number, has_side_effects=True, vmem_limit_bytes=48 * 1024 * 1024
@@ -465,7 +467,7 @@
     def _():
         for h in range(2):
             merged[:, 128 * h : 128 * h + 128] = merge_ref[256 * h : 256 * h + 256, :] * (1.0 / row_total)
-        parts = split(merged[...])
+        parts = split3(merged[...])
 
         def to_modes(block):
             inverse, _, _ = lower_inverse(fdot(times(block, parts), block, NT))
@@ -489,24 +491,23 @@
         factor[0:128, :] = high
         factor[128:, :] = low
 
-    high, low = split(joined_ref[...])
+    size = out_ref.shape[0]
+    here = pl.ds(pl.multiple_of(pl.program_id(0) * size, 128), size)
+    high, low = split(joined_ref[:, here])
     both = bdot(factor[...], high, NN)
     out_ref[...] = (both[:128] + both[128:] + bdot(factor[0:128, :], low, NN)).T
 
 
 def project(merge, start_merge, joined, row_total):
-    wide, rows = joined.shape
+    rows = joined.shape[1]
     return pl.pallas_call(
         functools.partial(project_kernel, row_total),
         grid=(rows // 512,),
-        in_specs=[
-            pl.BlockSpec((MERGE_ROWS, 128), lambda i: (0, 0)),
-            pl.BlockSpec((RANK, 256), lambda i: (0, 0)),
-            pl.BlockSpec((wide, 512), lambda i: (0, i)),
-        ],
+        in_specs=[VMEM, VMEM, VMEM],
         out_specs=pl.BlockSpec((512, 128), lambda i: (i, 0)),
         out_shape=jax.ShapeDtypeStruct((rows, 128), F32),
         scratch_shapes=[pltpu.VMEM((256, 256), F32), pltpu.VMEM((RANK, 256), F32), pltpu.VMEM((256, 256), BF16)],
+        compiler_params=pltpu.CompilerParams(vmem_limit_bytes=16 * 1024 * 1024),
         name="project",
     )(merge, start_merge, joined)
 

time: 177 us -> 165 us (0.932)
  Pallas kernels: 173 us -> 165 us
  local copies, waits for them, and re-layouts: 4.37 us -> 0.01 us
    pallas_call x1, Pallas kernels: 39.9 us -> 34.7 us  [project(): pl.pallas_call(functools.partial(project_kernel, row_total), grid=(rows /...]
    unnamed x10 -> x6, local copies, waits for them, and re-layouts: 4.37 us -> 0.01 us
    pallas_call x1, Pallas kernels: 31.6 us -> 27.8 us  [group_solve(): pl.pallas_call(functools.partial(solve_kernel, row_total), in_specs=[VMEM...]
where the time goes in v4:
time: 165 us
  Pallas kernels  165 us (100%)
    pallas_call x1, Pallas kernels, merged_over_rows(): pl.pallas_call(merge_kernel, in_specs=[VMEM, pl.BlockSpec(memory_space=pl...  61.8 us
    pallas_call x1, Pallas kernels, gram_over_rows(): pl.pallas_call(gram_kernel, in_specs=[pl.BlockSpec(memory_space=pl.ANY)],...  40.5 us
    pallas_call x1, Pallas kernels, project(): pl.pallas_call(functools.partial(project_kernel, row_total), grid=(rows /...  34.7 us
    pallas_call x1, Pallas kernels, group_solve(): pl.pallas_call(functools.partial(solve_kernel, row_total), in_specs=[VMEM...  27.8 us

profile of v4, /device:TPU:1, one launch (start us, length us, event | category | flops | bytes accessed | tf_op | source)
XLA Modules:
  0.0 164.8 jit_solution(17333880732998636019)
XLA Ops:
  0.0 0.0 copy-start.1
  0.0 0.0 copy-start
  0.0 40.5 %gram_over_rows.1.gram_ref = f32[1536,128]{1,0:T(8,128)S(1)} custom-call(f32[3584,512]{1,0:T(8,128)} %x_hbm.3), custom_call_target="tpu_custom_call" | custom-call | tf_op jit(solution)/shard_map/gram_over_rows/pallas_call | solution.py:292
  40.5 0.0 copy-done.1
  40.5 27.8 %group_solve.1.iterate_ref = f32[64,512]{1,0:T(8,128)S(1)} custom-call(f32[1536,128]{1,0:T(8,128)S(1)} %gram_over_rows.1.gram_ref, f32[64,512]{1,0:T(8,128)S(1)} %bitcast.2), custom_call_target="tpu_custom_call" | custom-call | tf_op jit(solution)/shard_map/group_solve/pallas_call | solution.py:330
  68.4 0.0 copy-done
  68.4 0.0 copy-start.2
  68.4 61.8 %merged_over_rows.1 = (f32[256,3584]{1,0:T(8,128)S(1)}, f32[1024,128]{1,0:T(8,128)S(1)}) custom-call(f32[64,512]{1,0:T(8,128)S(1)} %group_solve.1.iterate_ref, f32[3584,512]{1,0:T(8,128)} %x_hbm.3, f32[3584,128]{1,0:T(8,128)S(1)} %copy-done), custom_call_target="tpu_custom_call" | custom-call | tf_op jit(solution)/shard_map/merged_over_rows/pallas_call | solution.py:443
  130.2 0.0 copy-done.2
  130.2 34.7 %project.1 = f32[3584,128]{1,0:T(8,128)} custom-call(f32[1024,128]{1,0:T(8,128)S(1)} %get-tuple-element.7.merge_ref, f32[64,256]{1,0:T(8,128)S(1)} %bitcast.3, f32[256,3584]{1,0:T(8,128)S(1)} %get-tuple-element.8.joined_ref), custom_call_target="tpu_custom_call" | custom-call | tf_op jit(solution)/shard_map/project/pallas_call | solution.py:503
Async XLA Ops:
  0.0 40.5 %copy-start.1 = (f32[512,64]{0,1:T(8,128)S(1)}, f32[512,64]{0,1:T(8,128)}, u32[]{:S(2)}) copy-start(f32[512,64]{0,1:T(8,128)} %param.6) | copy-start | bytes 393220
  0.0 68.4 %copy-start = (f32[3584,128]{1,0:T(8,128)S(1)}, f32[3584,128]{1,0:T(8,128)}, u32[]{:S(2)}) copy-start(f32[3584,128]{1,0:T(8,128)} %test_ref.1) | copy-start | bytes 5505028
  68.4 61.8 %copy-start.2 = (f32[256,64]{0,1:T(8,128)S(1)}, f32[256,64]{0,1:T(8,128)}, u32[]{:S(2)}) copy-start(f32[256,64]{0,1:T(8,128)} %param.7) | copy-start | bytes 196612

commit v5 on v4

--- a/solution.py
+++ b/solution.py
@@ -46,9 +46,13 @@
     joint = jnp.concatenate([jnp.where(row == lane, 1.0, 0.0), small], axis=1)
     bands = [joint[8 * k : 8 * k + 8, :] for k in range(8)]
     done, least, most = [], None, None
+    corner = [spread(bands[0][:, 64 + c : 65 + c]) for c in range(8)]
     for k in range(8):
         first = 64 + 8 * k
-        cols = [[spread(bands[i][:, first + c : first + c + 1]) for c in range(8)] for i in range(k, 8)]
+        cols = [corner]
+        cols += [[spread(bands[i][:, first + c : first + c + 1]) for c in range(8)] for i in range(k + 1, 8)]
+        if k < 7:
+            corner = [spread(bands[k + 1][:, first + 8 + c : first + 9 + c]) for c in range(8)]
         line = [spread(bands[k][a : a + 1, :]) for a in range(8)]
         piv = [[spread(cols[0][c][a : a + 1, :]) for c in range(a + 1)] for a in range(8)]
         for a in range(8):
@@ -62,6 +66,8 @@
             for i in range(1, 8 - k):
                 share = cols[i][a] * inv
                 bands[k + i] = bands[k + i] - share * line[a]
+                if i == 1:
+                    corner = [corner[c] - share * spread(cols[1][a][c : c + 1, :]) for c in range(8)]
                 for c in range(a + 1, 8):
                     cols[i][c] = cols[i][c] - share * piv[c][a]
         band, diag = line[0], piv[0][0]
@@ -279,11 +285,8 @@
     work.begin(0)
     gram_second(high_ref, low_ref, part_ref)
     work.begin(1)
-    work.advance(0)
     gram_third(high_ref, low_ref, part_ref)
     work.begin(2)
-    work.advance(1)
-    work.advance(0)
     work.finish()
 
 
@@ -338,7 +341,7 @@
     )(gram, start_block)
 
 
-PIECES = 7
+PIECES = 4
 
 
 def merge_products(q, joined_ref, test_ref, first, second, third):

time: 165 us -> 148 us (0.90)
  Pallas kernels: 165 us -> 148 us
    pallas_call x1, Pallas kernels: 34.7 us -> 27.9 us  [project(): pl.pallas_call(functools.partial(project_kernel, row_total), grid=(rows /...]
    pallas_call x1, Pallas kernels: 27.8 us -> 22.3 us  [group_solve(): pl.pallas_call(functools.partial(solve_kernel, row_total), in_specs=[VMEM...]
    pallas_call x1, Pallas kernels: 40.5 us -> 36.6 us  [gram_over_rows(): pl.pallas_call(gram_kernel, in_specs=[pl.BlockSpec(memory_space=pl.ANY)],...]
where the time goes in v5:
time: 148 us
  Pallas kernels  148 us (100%)
    pallas_call x1, Pallas kernels, merged_over_rows(): pl.pallas_call(merge_kernel, in_specs=[VMEM, pl.BlockSpec(memory_space=pl...  60.8 us
    pallas_call x1, Pallas kernels, gram_over_rows(): pl.pallas_call(gram_kernel, in_specs=[pl.BlockSpec(memory_space=pl.ANY)],...  36.6 us
    pallas_call x1, Pallas kernels, project(): pl.pallas_call(functools.partial(project_kernel, row_total), grid=(rows /...  27.9 us
    pallas_call x1, Pallas kernels, group_solve(): pl.pallas_call(functools.partial(solve_kernel, row_total), in_specs=[VMEM...  22.3 us

profile of v5, /device:TPU:1, one launch (start us, length us, event | category | flops | bytes accessed | tf_op | source)
XLA Modules:
  0.0 147.6 jit_solution(390600846354893876)
XLA Ops:
  0.0 0.0 copy-start.1
  0.0 0.0 copy-start
  0.0 36.6 %gram_over_rows.1.gram_ref = f32[1536,128]{1,0:T(8,128)S(1)} custom-call(f32[3584,512]{1,0:T(8,128)} %x_hbm.3), custom_call_target="tpu_custom_call" | custom-call | tf_op jit(solution)/shard_map/gram_over_rows/pallas_call | solution.py:295
  36.6 0.0 copy-done.1
  36.6 22.3 %group_solve.1.iterate_ref = f32[64,512]{1,0:T(8,128)S(1)} custom-call(f32[1536,128]{1,0:T(8,128)S(1)} %gram_over_rows.1.gram_ref, f32[64,512]{1,0:T(8,128)S(1)} %bitcast.2), custom_call_target="tpu_custom_call" | custom-call | tf_op jit(solution)/shard_map/group_solve/pallas_call | solution.py:333
  58.9 0.0 copy-done
  58.9 0.0 copy-start.2
  58.9 60.8 %merged_over_rows.1 = (f32[256,3584]{1,0:T(8,128)S(1)}, f32[1024,128]{1,0:T(8,128)S(1)}) custom-call(f32[64,512]{1,0:T(8,128)S(1)} %group_solve.1.iterate_ref, f32[3584,512]{1,0:T(8,128)} %x_hbm.3, f32[3584,128]{1,0:T(8,128)S(1)} %copy-done), custom_call_target="tpu_custom_call" | custom-call | tf_op jit(solution)/shard_map/merged_over_rows/pallas_call | solution.py:446
  119.7 0.0 copy-done.2
  119.7 27.9 %project.1 = f32[3584,128]{1,0:T(8,128)} custom-call(f32[1024,128]{1,0:T(8,128)S(1)} %get-tuple-element.7.merge_ref, f32[64,256]{1,0:T(8,128)S(1)} %bitcast.3, f32[256,3584]{1,0:T(8,128)S(1)} %get-tuple-element.8.joined_ref), custom_call_target="tpu_custom_call" | custom-call | tf_op jit(solution)/shard_map/project/pallas_call | solution.py:506
Async XLA Ops:
  0.0 36.6 %copy-start.1 = (f32[512,64]{0,1:T(8,128)S(1)}, f32[512,64]{0,1:T(8,128)}, u32[]{:S(2)}) copy-start(f32[512,64]{0,1:T(8,128)} %param.6) | copy-start | bytes 393220
  0.0 58.9 %copy-start = (f32[3584,128]{1,0:T(8,128)S(1)}, f32[3584,128]{1,0:T(8,128)}, u32[]{:S(2)}) copy-start(f32[3584,128]{1,0:T(8,128)} %test_ref.1) | copy-start | bytes 5505028
  58.9 60.8 %copy-start.2 = (f32[256,64]{0,1:T(8,128)S(1)}, f32[256,64]{0,1:T(8,128)}, u32[]{:S(2)}) copy-start(f32[256,64]{0,1:T(8,128)} %param.7) | copy-start | bytes 196612

commit v6 on v5

--- a/solution.py
+++ b/solution.py
@@ -146,12 +146,10 @@
     pl.semaphore_wait(pltpu.get_barrier_semaphore(), len(peers))
 
 
-def pieces_in(src, dst, sem):
-    count = sem.shape[0]
-    part = src.shape[0] // count
+def pieces_in(src, dst, sem, cuts):
     made = [
-        pltpu.make_async_copy(src.at[pl.ds(q * part, part)], dst.at[pl.ds(q * part, part)], sem.at[q])
-        for q in range(count)
+        pltpu.make_async_copy(src.at[pl.ds(at, size)], dst.at[pl.ds(at, size)], sem.at[q])
+        for q, (at, size) in enumerate(cuts)
     ]
     for one in made:
         one.start()
@@ -278,7 +276,8 @@
 def gram_kernel(x_hbm, out_ref, x_ref, high_ref, low_ref, part_ref, x_sem, *scratch):
     work = StagedSum(part_ref, out_ref, *scratch)
     peers = [work.mate] + [peer for _, peer in work.along_y + work.along_z]
-    x_pieces = pieces_in(x_hbm, x_ref, x_sem)
+    part = x_ref.shape[0] // 4
+    x_pieces = pieces_in(x_hbm, x_ref, x_sem, [(q * part, part) for q in range(4)])
     greet(peers)
     gram_first(x_pieces, x_ref, high_ref, low_ref, part_ref)
     meet(peers)
@@ -341,13 +340,19 @@
     )(gram, start_block)
 
 
-PIECES = 4
+SHARES = (4, 7, 7, 7, 3)
+PIECES = len(SHARES)
+
+
+def row_cuts(rows):
+    unit = rows // sum(SHARES)
+    return [(unit * sum(SHARES[:q]), unit * SHARES[q]) for q in range(PIECES)]
 
 
 def merge_products(q, joined_ref, test_ref, first, second, third):
-    part = test_ref.shape[0] // PIECES
-    high, low = split(joined_ref[:, q * part : (q + 1) * part])
-    test_high, test_low = split(test_ref[q * part : (q + 1) * part, :])
+    at, size = row_cuts(test_ref.shape[0])[q]
+    high, low = split(joined_ref[:, at : at + size])
+    test_high, test_low = split(test_ref[at : at + size, :])
     one = bdot(high, high, NT)
     two = bdot(high, low, NT)
     three = bdot(high, test_high, NN) + bdot(high, test_low, NN) + bdot(low, test_high, NN)
@@ -371,15 +376,15 @@
     g = lax.axis_index("grp")
     y, z, c = (lax.axis_index(name) for name in ROW)
     right, left = lax.rem(g + 1, 4), lax.rem(g + 3, 4)
-    part = x_ref.shape[0] // PIECES
-    x_pieces = pieces_in(x_hbm, x_ref, x_sem)
+    cuts = row_cuts(x_ref.shape[0])
+    x_pieces = pieces_in(x_hbm, x_ref, x_sem, cuts)
     work = StagedSum(part_ref, merge_ref, *scratch)
     peers = [(right, y, z, c), (left, y, z, c), work.mate] + [peer for _, peer in work.along_y + work.along_z]
     greet(peers)
     high_low = jnp.concatenate(split(iterate_ref[...]), axis=0)
 
     def place(block, q, first_row, size):
-        return out_ref.at[rows_at(block * RANK + first_row, size), pl.ds(q * part, part)]
+        return out_ref.at[rows_at(block * RANK + first_row, size), pl.ds(*cuts[q])]
 
     def own(q):
         return [
@@ -405,9 +410,8 @@
 
     def make(q):
         x_pieces[q].wait()
-        out_ref[rows_at(g * RANK, RANK), q * part : (q + 1) * part] = basis_piece(
-            high_low, x_ref[q * part : (q + 1) * part, :]
-        )
+        at, size = cuts[q]
+        out_ref[rows_at(g * RANK, RANK), at : at + size] = basis_piece(high_low, x_ref[at : at + size, :])
 
     make(0)
     meet(peers)

time: 148 us -> 148 us (level)
  no operation moved by 1% of the time
where the time goes in v6:
time: 148 us
  Pallas kernels  148 us (100%)
    pallas_call x1, Pallas kernels, merged_over_rows(): pl.pallas_call(merge_kernel, in_specs=[VMEM, pl.BlockSpec(memory_space=pl...  60.8 us
    pallas_call x1, Pallas kernels, gram_over_rows(): pl.pallas_call(gram_kernel, in_specs=[pl.BlockSpec(memory_space=pl.ANY)],...  36.6 us
    pallas_call x1, Pallas kernels, project(): pl.pallas_call(functools.partial(project_kernel, row_total), grid=(rows /...  27.9 us
    pallas_call x1, Pallas kernels, group_solve(): pl.pallas_call(functools.partial(solve_kernel, row_total), in_specs=[VMEM...  22.3 us

profile of v6, /device:TPU:1, one launch (start us, length us, event | category | flops | bytes accessed | tf_op | source)
XLA Modules:
  0.0 147.6 jit_solution(5992400806412034284)
XLA Ops:
  0.0 0.0 copy-start.1
  0.0 0.0 copy-start
  0.0 36.6 %gram_over_rows.1.gram_ref = f32[1536,128]{1,0:T(8,128)S(1)} custom-call(f32[3584,512]{1,0:T(8,128)} %x_hbm.3), custom_call_target="tpu_custom_call" | custom-call | tf_op jit(solution)/shard_map/gram_over_rows/pallas_call | solution.py:294
  36.6 0.0 copy-done.1
  36.6 22.3 %group_solve.1.iterate_ref = f32[64,512]{1,0:T(8,128)S(1)} custom-call(f32[1536,128]{1,0:T(8,128)S(1)} %gram_over_rows.1.gram_ref, f32[64,512]{1,0:T(8,128)S(1)} %bitcast.2), custom_call_target="tpu_custom_call" | custom-call | tf_op jit(solution)/shard_map/group_solve/pallas_call | solution.py:332
  58.9 0.0 copy-done
  58.9 0.0 copy-start.2
  58.9 60.8 %merged_over_rows.1 = (f32[256,3584]{1,0:T(8,128)S(1)}, f32[1024,128]{1,0:T(8,128)S(1)}) custom-call(f32[64,512]{1,0:T(8,128)S(1)} %group_solve.1.iterate_ref, f32[3584,512]{1,0:T(8,128)} %x_hbm.3, f32[3584,128]{1,0:T(8,128)S(1)} %copy-done), custom_call_target="tpu_custom_call" | custom-call | tf_op jit(solution)/shard_map/merged_over_rows/pallas_call | solution.py:450
  119.7 0.0 copy-done.2
  119.8 27.9 %project.1 = f32[3584,128]{1,0:T(8,128)} custom-call(f32[1024,128]{1,0:T(8,128)S(1)} %get-tuple-element.7.merge_ref, f32[64,256]{1,0:T(8,128)S(1)} %bitcast.3, f32[256,3584]{1,0:T(8,128)S(1)} %get-tuple-element.8.joined_ref), custom_call_target="tpu_custom_call" | custom-call | tf_op jit(solution)/shard_map/project/pallas_call | solution.py:510
Async XLA Ops:
  0.0 36.6 %copy-start.1 = (f32[512,64]{0,1:T(8,128)S(1)}, f32[512,64]{0,1:T(8,128)}, u32[]{:S(2)}) copy-start(f32[512,64]{0,1:T(8,128)} %param.6) | copy-start | bytes 393220
  0.0 58.9 %copy-start = (f32[3584,128]{1,0:T(8,128)S(1)}, f32[3584,128]{1,0:T(8,128)}, u32[]{:S(2)}) copy-start(f32[3584,128]{1,0:T(8,128)} %test_ref.1) | copy-start | bytes 5505028
  58.9 60.8 %copy-start.2 = (f32[256,64]{0,1:T(8,128)S(1)}, f32[256,64]{0,1:T(8,128)}, u32[]{:S(2)}) copy-start(f32[256,64]{0,1:T(8,128)} %param.7) | copy-start | bytes 196612

commit v7 on v5

--- a/solution.py
+++ b/solution.py
@@ -505,9 +505,9 @@
     rows = joined.shape[1]
     return pl.pallas_call(
         functools.partial(project_kernel, row_total),
-        grid=(rows // 512,),
+        grid=(rows // 896,),
         in_specs=[VMEM, VMEM, VMEM],
-        out_specs=pl.BlockSpec((512, 128), lambda i: (i, 0)),
+        out_specs=pl.BlockSpec((896, 128), lambda i: (i, 0)),
         out_shape=jax.ShapeDtypeStruct((rows, 128), F32),
         scratch_shapes=[pltpu.VMEM((256, 256), F32), pltpu.VMEM((RANK, 256), F32), pltpu.VMEM((256, 256), BF16)],
         compiler_params=pltpu.CompilerParams(vmem_limit_bytes=16 * 1024 * 1024),

time: 148 us -> 146 us (0.986)
  Pallas kernels: 148 us -> 146 us
where the time goes in v7:
time: 146 us
  Pallas kernels  146 us (100%)
    pallas_call x1, Pallas kernels, merged_over_rows(): pl.pallas_call(merge_kernel, in_specs=[VMEM, pl.BlockSpec(memory_space=pl...  60.8 us
    pallas_call x1, Pallas kernels, gram_over_rows(): pl.pallas_call(gram_kernel, in_specs=[pl.BlockSpec(memory_space=pl.ANY)],...  36.6 us
    pallas_call x1, Pallas kernels, project(): pl.pallas_call(functools.partial(project_kernel, row_total), grid=(rows /...  26.7 us
    pallas_call x1, Pallas kernels, group_solve(): pl.pallas_call(functools.partial(solve_kernel, row_total), in_specs=[VMEM...  22.3 us

profile of v7, /device:TPU:1, one launch (start us, length us, event | category | flops | bytes accessed | tf_op | source)
XLA Modules:
  0.0 146.4 jit_solution(5786341074293106538)
XLA Ops:
  0.0 0.0 copy-start.1
  0.0 0.0 copy-start
  0.0 36.6 %gram_over_rows.1.gram_ref = f32[1536,128]{1,0:T(8,128)S(1)} custom-call(f32[3584,512]{1,0:T(8,128)} %x_hbm.3), custom_call_target="tpu_custom_call" | custom-call | tf_op jit(solution)/shard_map/gram_over_rows/pallas_call | solution.py:295
  36.6 0.0 copy-done.1
  36.6 22.3 %group_solve.1.iterate_ref = f32[64,512]{1,0:T(8,128)S(1)} custom-call(f32[1536,128]{1,0:T(8,128)S(1)} %gram_over_rows.1.gram_ref, f32[64,512]{1,0:T(8,128)S(1)} %bitcast.2), custom_call_target="tpu_custom_call" | custom-call | tf_op jit(solution)/shard_map/group_solve/pallas_call | solution.py:333
  58.9 0.0 copy-done
  58.9 0.0 copy-start.2
  58.9 60.8 %merged_over_rows.1 = (f32[256,3584]{1,0:T(8,128)S(1)}, f32[1024,128]{1,0:T(8,128)S(1)}) custom-call(f32[64,512]{1,0:T(8,128)S(1)} %group_solve.1.iterate_ref, f32[3584,512]{1,0:T(8,128)} %x_hbm.3, f32[3584,128]{1,0:T(8,128)S(1)} %copy-done), custom_call_target="tpu_custom_call" | custom-call | tf_op jit(solution)/shard_map/merged_over_rows/pallas_call | solution.py:446
  119.7 0.0 copy-done.2
  119.7 26.7 %project.1 = f32[3584,128]{1,0:T(8,128)} custom-call(f32[1024,128]{1,0:T(8,128)S(1)} %get-tuple-element.7.merge_ref, f32[64,256]{1,0:T(8,128)S(1)} %bitcast.3, f32[256,3584]{1,0:T(8,128)S(1)} %get-tuple-element.8.joined_ref), custom_call_target="tpu_custom_call" | custom-call | tf_op jit(solution)/shard_map/project/pallas_call | solution.py:506
Async XLA Ops:
  0.0 36.6 %copy-start.1 = (f32[512,64]{0,1:T(8,128)S(1)}, f32[512,64]{0,1:T(8,128)}, u32[]{:S(2)}) copy-start(f32[512,64]{0,1:T(8,128)} %param.6) | copy-start | bytes 393220
  0.0 58.9 %copy-start = (f32[3584,128]{1,0:T(8,128)S(1)}, f32[3584,128]{1,0:T(8,128)}, u32[]{:S(2)}) copy-start(f32[3584,128]{1,0:T(8,128)} %test_ref.1) | copy-start | bytes 5505028
  58.9 60.8 %copy-start.2 = (f32[256,64]{0,1:T(8,128)S(1)}, f32[256,64]{0,1:T(8,128)}, u32[]{:S(2)}) copy-start(f32[256,64]{0,1:T(8,128)} %param.7) | copy-start | bytes 196612
